TPU v7x, 32 devices: a whole 2x2x4 slice. The times are simulated.
32 devices in a mesh: stack: 2 (over y), date: 4 (over x, core), line: 4 (over z).
Axes of the slice: x: 2, y: 2, z: 4, core: 2. Of those that a mesh axis runs over, the one named last changes fastest.
Arguments:
- slc: float32 [4, 2, 512, 1280], P('date', None, 'stack', 'line'), parts along dimension 2, may hold values from -6 to 6
- band_start: int32 [4], replicated, may hold values from 0 to 640, as said below
- band_stop: int32 [4], replicated, may hold values from 640 to 1280, as said below
Outputs:
- interferogram: float32 [4, 2, 512, 256], P('date', None, 'stack', 'line'), parts along dimension 2
There are 2 independent parts, one for each index of `stack`. A program takes and returns all parts, laid end to end along the dimension named above; an argument that names none is the same for every part. Nothing has to cross between parts.
Inputs may be any that keep to these rules, and one draw needn't show every extreme that they name: For every pair, band_stop - band_start lies between 640 and 960; at least one pair keeps exactly 960 bins, and some pair keeps exactly 640 bins ending at 1280. `band_stop`: see band_start.
All inputs are finite; a program needn't handle non-finite values.
Results may differ from a plain program's by a relative error of at most 0.0001.
Values sent between devices are 32-bit elements; how exact they have to be, the bound alone decides.
No kernel may reach another device: no remote copies, remote signals or barrier semaphores. Data moves between devices by JAX's collectives and lax.ppermute only.
A program may use at most 64 MiB of HBM per device.

v0:
```python
import functools
import math

import jax
import jax.numpy as jnp
import numpy as np
from jax import lax
from jax.experimental import pallas as pl
from jax.experimental.pallas import tpu as pltpu
from jax.sharding import PartitionSpec as P


LOOKS = 5
TAPS = 2 * LOOKS
EXCHANGE = ((3, 2, 1, 0), (1, 0, 3, 2), (2, 3, 0, 1))
RETURN = ((2, 3, 0, 1), (3, 2, 1, 0), (1, 0, 3, 2))
LANES = 128
MIB = 1 << 20
HALF = LANES // 2


HIGHEST_PRECISION = lax.Precision.HIGHEST


def shifted(shard, axis, by):
    size = lax.axis_size(axis)
    return lax.ppermute(shard, axis, [(i, (i + by) % size) for i in range(size)])


def phase_table(count, sign_value):
    index_row = jnp.arange(count, dtype=jnp.int32)
    wrapped = index_row[:, None] * index_row[None, :] % count
    angle_all = 2.0 * math.pi / count * wrapped.astype(jnp.float32)
    return (jnp.cos(angle_all), sign_value * jnp.sin(angle_all))


def twiddle_table(outer, inner, sign_value):
    outer_row = jnp.arange(outer, dtype=jnp.int32)
    inner_row = jnp.arange(inner, dtype=jnp.int32)
    wrapped = outer_row[:, None] * inner_row[None, :] % (outer * inner)
    angle_all = 2.0 * math.pi / (outer * inner) * wrapped.astype(jnp.float32)
    return (jnp.cos(angle_all), sign_value * jnp.sin(angle_all))


def left_product(table_real, table_imag, data_real, data_imag):

    def single(table, data):
        return jnp.einsum("ka,cab->ckb", table, data, precision=HIGHEST_PRECISION)

    return (
        single(table_real, data_real) - single(table_imag, data_imag),
        single(table_real, data_imag) + single(table_imag, data_real),
    )


def right_product(data_real, data_imag, table_real, table_imag):

    def single(data, table):
        return jnp.einsum("ckb,bm->ckm", data, table, precision=HIGHEST_PRECISION)

    return (
        single(data_real, table_real) - single(data_imag, table_imag),
        single(data_imag, table_real) + single(data_real, table_imag),
    )


def forward_dft(data_real, data_imag):
    outer = data_real.shape[1]
    inner = data_real.shape[2]
    outer_real, outer_imag = phase_table(outer, -1.0)
    first_real, first_imag = left_product(outer_real, outer_imag, data_real, data_imag)
    twist_real, twist_imag = twiddle_table(outer, inner, -1.0)
    turned_real = first_real * twist_real - first_imag * twist_imag
    turned_imag = first_real * twist_imag + first_imag * twist_real
    inner_real, inner_imag = phase_table(inner, -1.0)
    return right_product(turned_real, turned_imag, inner_real, inner_imag)


def inverse_dft(data_real, data_imag):
    outer = data_real.shape[1]
    inner = data_real.shape[2]
    inner_real, inner_imag = phase_table(inner, 1.0)
    first_real, first_imag = right_product(data_real, data_imag, inner_real, inner_imag)
    twist_real, twist_imag = twiddle_table(outer, inner, 1.0)
    turned_real = first_real * twist_real - first_imag * twist_imag
    turned_imag = first_real * twist_imag + first_imag * twist_real
    outer_real, outer_imag = phase_table(outer, 1.0)
    result_real, result_imag = left_product(outer_real, outer_imag, turned_real, turned_imag)
    scale = 1.0 / (outer * inner)
    return (result_real * scale, result_imag * scale)


def conj_product(ref_real, ref_imag, sec_real, sec_imag):
    return (ref_real * sec_real + ref_imag * sec_imag, ref_imag * sec_real - ref_real * sec_imag)


def look_mean(values):
    return values.reshape(values.shape[0], values.shape[1] // LOOKS, LOOKS).sum(axis=-1) * (
        1.0 / LOOKS
    )


def general_shards(slc, band_start, band_stop):
    own_image = slc[0]
    line_lines = own_image.shape[2]
    turned = lax.all_to_all(own_image, "line", split_axis=1, concat_axis=2, tiled=True)
    columns = turned.shape[1]
    outer = lax.axis_size("line")
    lines_all = outer * line_lines
    blocks = turned.reshape(2, columns, outer, line_lines)
    spec_real, spec_imag = forward_dft(blocks[0], blocks[1])
    spectrum = jnp.stack([spec_real, spec_imag], axis=0)
    date_index = lax.axis_index("date")
    my_start = lax.dynamic_slice_in_dim(band_start, date_index, 1)[0]
    my_end = lax.dynamic_slice_in_dim(band_stop, date_index, 1)[0]
    bin_index = (
        jnp.arange(outer, dtype=jnp.int32)[:, None]
        + outer * jnp.arange(line_lines, dtype=jnp.int32)[None, :]
    )
    keep_mask = ((bin_index >= my_start) & (bin_index < my_end)).astype(jnp.float32)
    partner = shifted(spectrum, "date", -1)
    ref_spec = spectrum * keep_mask
    sec_spec = partner * keep_mask
    both_real, both_imag = inverse_dft(
        jnp.concatenate([ref_spec[0], sec_spec[0]], axis=0),
        jnp.concatenate([ref_spec[1], sec_spec[1]], axis=0),
    )
    ref_real = both_real[:columns].reshape(columns, lines_all)
    ref_imag = both_imag[:columns].reshape(columns, lines_all)
    sec_real = both_real[columns:].reshape(columns, lines_all)
    sec_imag = both_imag[columns:].reshape(columns, lines_all)
    prod_real, prod_imag = conj_product(ref_real, ref_imag, sec_real, sec_imag)
    looked = jnp.stack([look_mean(prod_real), look_mean(prod_imag)], axis=0)
    result = lax.all_to_all(looked, "line", split_axis=2, concat_axis=1, tiled=True)
    return result[None]


def split_pair(values):
    high = values.astype(jnp.bfloat16)
    low = (values - high.astype(jnp.float32)).astype(jnp.bfloat16)
    return high, low


@functools.lru_cache(maxsize=None)
def host_tables(inner, first_step, few):
    lines_all = TAPS * inner
    bins, steps, taps = np.arange(inner), np.arange(inner), np.arange(TAPS)
    turns = bins[None, :, None] * (TAPS * steps[None, None, :] + taps[:, None, None]) % lines_all
    angle = 2.0 * np.pi / lines_all * turns
    cos, sin = np.cos(angle), np.sin(angle)

    def halves(table):
        high = table.astype(jnp.bfloat16)
        low = (table - high.astype(np.float64)).astype(jnp.bfloat16)
        return high, low

    ahead = halves(np.concatenate([cos, sin], axis=2))
    swapped = [np.swapaxes(table, 1, 2) for table in (cos, -sin)]
    back = halves(np.concatenate(swapped, axis=2))
    part = slice(first_step, first_step + few)
    high, low = halves(np.concatenate([cos[:, :, part], sin[:, :, part]], axis=2))
    late = np.concatenate([high, high, low], axis=2)
    late = np.pad(late, ((0, 0), (0, 0), (0, -late.shape[2] % LANES)))
    return np.stack(ahead), np.stack(back), late


def low_lanes(shape):
    return lax.broadcasted_iota(jnp.int32, shape, len(shape) - 1) < HALF


def swap_halves(values):
    return pltpu.roll(values, HALF, values.ndim - 1)


def turned(values):
    other = swap_halves(values)
    return jnp.where(low_lanes(values.shape), other, -other)


def entry(row, me):
    code = sum(value << (4 * place) for place, value in enumerate(row))
    return jnp.bitwise_and(jnp.right_shift(jnp.int32(code), 4 * me), 15)


def senders(row):
    return tuple(row.index(place) for place in range(len(row)))


def pack_kernel(image_ref, *chunk_refs):
    me = lax.axis_index("line")
    for row, chunk_ref in zip((None,) + EXCHANGE, chunk_refs):
        block = me if row is None else entry(row, me)
        lane = pl.multiple_of(block // 2 * LANES, LANES)
        side = block % 2
        stay = image_ref[side, :, pl.ds(lane, LANES)]
        move = image_ref[1 - side, :, pl.ds(lane, LANES)]
        half = lax.broadcasted_iota(jnp.int32, stay.shape, 1) // HALF
        chunk_ref[...] = jnp.where(half == side, stay, swap_halves(move))


COS1, COS2 = math.cos(2.0 * math.pi / 5), math.cos(4.0 * math.pi / 5)
SIN1, SIN2 = math.sin(2.0 * math.pi / 5), math.sin(4.0 * math.pi / 5)


def five_point(x, sign):
    unit = jnp.where(low_lanes(x[0].shape), sign, -sign)
    sin1, sin2 = SIN1 * unit, SIN2 * unit
    sum1, sum2 = x[1] + x[4], x[2] + x[3]
    dif1, dif2 = x[1] - x[4], x[2] - x[3]
    even1 = x[0] + COS1 * sum1 + COS2 * sum2
    even2 = x[0] + COS2 * sum1 + COS1 * sum2
    odd1 = swap_halves(sin1 * dif1 + sin2 * dif2)
    odd2 = swap_halves(sin2 * dif1 - sin1 * dif2)
    return [x[0] + sum1 + sum2, even1 + odd1, even2 + odd2, even2 - odd2, even1 - odd1]


def ten_point(x, sign):
    first = [x[2 * b % TAPS] for b in range(LOOKS)]
    other = [x[(LOOKS + 2 * b) % TAPS] for b in range(LOOKS)]
    even = five_point([p + q for p, q in zip(first, other)], sign)
    odd = five_point([p - q for p, q in zip(first, other)], sign)
    return [(odd if m % 2 else even)[m % LOOKS] for m in range(TAPS)]


def block_of(me, block, peers):
    return (block - entry(senders(EXCHANGE[-1]), me)) % peers


def product(table, data):
    return jnp.dot(table, data, preferred_element_type=jnp.float32)


def stacked(*values):
    return jnp.concatenate(values, axis=0)


def beside(*values):
    return jnp.concatenate(values, axis=1)


def spectral(mid_ref, weight_ref, back_ref):
    rows = 8

    def block(step, carry):
        span = pl.ds(pl.multiple_of(step * rows, rows), rows)
        x = ten_point([mid_ref[l, span, :] for l in range(TAPS)], -1.0)
        x = ten_point([x[m] * weight_ref[m, span, :] for m in range(TAPS)], 1.0)
        for l in range(TAPS):
            back_ref[l, span, :] = x[l]
        return carry

    lax.fori_loop(0, mid_ref.shape[1] // rows, block, 0, unroll=True)


def signal_of(mid_ref, back_ref, l):
    values = mid_ref[l]
    high, low = split_pair(stacked(values, turned(values)))
    both = beside(high, low)
    signal = product(back_ref[0, l], both) + product(back_ref[1, l], both)
    return signal[:, :LANES] + signal[:, LANES:]


def tables_kernel(count, *refs):
    for source, target in zip(refs[:count], refs[count:]):
        target[...] = source[...]


def early_kernel(peers, start_ref, stop_ref, ahead_ref, back_ref, *refs):
    own_refs, sec_refs = refs[:peers], refs[peers : 2 * peers - 1]
    mid_ref, weight_ref, same_ref, cross_ref = refs[2 * peers - 1 : 2 * peers + 3]
    own_ref, own_turned_ref, sec_ref, sec_turned_ref = refs[2 * peers + 3 : -2]
    own_mid_ref, own_back_ref = refs[-2:]
    me = lax.axis_index("line")
    date = lax.axis_index("date")
    lines = own_ref.shape[0] // peers
    inner = own_ref.shape[0] // TAPS
    for q in range(peers):
        block = entry(senders(EXCHANGE[q - 1]), me) if q else me
        span = pl.ds(pl.multiple_of(block_of(me, block, peers) * lines, 8), lines)
        own = own_refs[q][...]
        own_ref[span, :] = own
        own_turned_ref[span, :] = turned(own)
        if q == peers - 1:
            sec_ref[span, :] = jnp.zeros((lines, LANES), jnp.float32)
            sec_turned_ref[span, :] = jnp.zeros((lines, LANES), jnp.float32)
        else:
            sec = sec_refs[q][...]
            sec_ref[span, :] = sec
            sec_turned_ref[span, :] = turned(sec)
    for l in range(TAPS):
        span = pl.ds(l, inner, stride=TAPS)
        high, low = split_pair(
            stacked(
                beside(own_ref[span, :], sec_ref[span, :]),
                beside(own_turned_ref[span, :], sec_turned_ref[span, :]),
            )
        )
        table_high, table_low = ahead_ref[0, l], ahead_ref[1, l]
        bins = product(table_high, high) + product(table_low, high) + product(table_high, low)
        own_mid_ref[l] = bins[:, :LANES]
        mid_ref[l] = bins[:, LANES:]

    first, stop = start_ref[date], stop_ref[date]
    for m in range(TAPS):
        bin_index = lax.broadcasted_iota(jnp.int32, (inner, LANES), 0) + m * inner
        keep = (bin_index >= first) & (bin_index < stop)
        weight_ref[m] = jnp.where(keep, 1.0 / (TAPS * inner), 0.0)
    spectral(own_mid_ref, weight_ref, own_back_ref)
    for l in range(TAPS):
        signal = signal_of(own_back_ref, back_ref, l) * (1.0 / LOOKS)
        other = swap_halves(signal)
        mask = low_lanes(signal.shape)
        same_ref[l] = jnp.where(mask, signal, -other)
        cross_ref[l] = jnp.where(mask, other, signal)


def late_kernel(
    peers, late_ref, back_ref, mid_ref, weight_ref, same_ref, cross_ref, sec_ref, *refs
):
    out_refs = refs[:peers]
    total_ref, taps_ref, sum_ref = refs[peers:]
    me = lax.axis_index("line")
    inner = mid_ref.shape[1]
    few = sec_ref.shape[0] // TAPS
    rest = jnp.zeros((late_ref.shape[2] - 6 * few, LANES), jnp.bfloat16)
    for l in range(TAPS):
        span = pl.ds(l, few, stride=TAPS)
        values = sec_ref[span, :]
        high, low = split_pair(stacked(values, turned(values)))
        total_ref[l] = mid_ref[l] + product(late_ref[l], stacked(high, low, high, rest))
    spectral(total_ref, weight_ref, taps_ref)
    for half in range(2):
        same, cross = None, None
        for l in range(half * LOOKS, (half + 1) * LOOKS):
            signal = signal_of(taps_ref, back_ref, l)
            new_same, new_cross = same_ref[l] * signal, cross_ref[l] * signal
            same = new_same if same is None else same + new_same
            cross = new_cross if cross is None else cross + new_cross
        sum_ref[pl.ds(half, inner, stride=2), :] = same + swap_halves(cross)
    out_lines = 2 * inner // peers
    for q in range(peers):
        block = entry(RETURN[q - 1], me) if q else me
        base = pl.multiple_of(block_of(me, block, peers) * out_lines, 8)
        out_refs[q][...] = sum_ref[pl.ds(base, out_lines), :]


def unpack_kernel(peers, *refs):
    chunk_refs, (out_ref, held_ref) = refs[:peers], refs[peers:]
    me = lax.axis_index("line")
    for q in range(peers):
        held_ref[entry(senders(RETURN[q - 1]), me) if q else me] = chunk_refs[q][...]
    for pair in range(peers // 2):
        span = slice(pair * LANES, (pair + 1) * LANES)
        first, second = held_ref[2 * pair], held_ref[2 * pair + 1]
        mask = low_lanes(first.shape)
        out_ref[0, :, span] = jnp.where(mask, first, swap_halves(second))
        out_ref[1, :, span] = jnp.where(mask, swap_halves(first), second)


def packed_step(slc, band_start, band_stop):
    peers = lax.axis_size("line")
    chunk_lines = slc.shape[3]
    inner = peers * chunk_lines // TAPS
    out_lines = 2 * inner // peers
    f32 = jnp.float32
    vmem = pl.BlockSpec(memory_space=pltpu.VMEM)
    smem = pl.BlockSpec(memory_space=pltpu.SMEM)
    params = pltpu.CompilerParams(vmem_limit_bytes=16 * MIB)
    image = jnp.transpose(slc[0], (0, 2, 1))
    packed = pl.pallas_call(
        pack_kernel,
        out_shape=[jax.ShapeDtypeStruct((chunk_lines, LANES), f32)] * peers,
        in_specs=[vmem],
        out_specs=[vmem] * peers,
        compiler_params=pltpu.CompilerParams(vmem_limit_bytes=8 * MIB),
        name="pack",
    )(image)

    def exchange(values, row):
        return lax.ppermute(values, "line", list(enumerate(row)))

    def forward(values):
        return shifted(values, "date", -1)

    own = [
        exchange(values, EXCHANGE[q - 1]) if q else values
        for q, values in enumerate(packed)
    ]
    sec = [forward(values) for values in own]
    tables = [jnp.asarray(table) for table in host_tables(inner, 0, chunk_lines // TAPS)]
    ahead_table, back_table, late_table = pl.pallas_call(
        functools.partial(tables_kernel, len(tables)),
        out_shape=[jax.ShapeDtypeStruct(table.shape, table.dtype) for table in tables],
        in_specs=[vmem] * len(tables),
        out_specs=[vmem] * len(tables),
        compiler_params=params,
        name="tables",
    )(*tables)
    taps = jax.ShapeDtypeStruct((TAPS, inner, LANES), f32)
    plane = pltpu.VMEM((peers * chunk_lines, LANES), f32)
    middle, weight, same, cross = pl.pallas_call(
        functools.partial(early_kernel, peers),
        out_shape=[taps] * 4,
        in_specs=[smem, smem] + [vmem] * (2 * peers + 1),
        out_specs=[vmem] * 4,
        scratch_shapes=[plane] * 4 + [pltpu.VMEM(taps.shape, f32)] * 2,
        compiler_params=params,
        name="early",
    )(band_start, band_stop, ahead_table, back_table, *own, *sec[:-1])
    looked = pl.pallas_call(
        functools.partial(late_kernel, peers),
        out_shape=[jax.ShapeDtypeStruct((out_lines, LANES), f32)] * peers,
        in_specs=[vmem] * 7,
        out_specs=[vmem] * peers,
        scratch_shapes=[
            pltpu.VMEM(taps.shape, f32),
            pltpu.VMEM(taps.shape, f32),
            pltpu.VMEM((2 * inner, LANES), f32),
        ],
        compiler_params=params,
        name="late",
    )(late_table, back_table, middle, weight, same, cross, sec[-1])
    looked = [
        exchange(values, RETURN[q - 1]) if q else values
        for q, values in enumerate(looked)
    ]
    result = pl.pallas_call(
        functools.partial(unpack_kernel, peers),
        out_shape=jax.ShapeDtypeStruct((2, out_lines, slc.shape[2]), f32),
        in_specs=[vmem] * peers,
        out_specs=vmem,
        scratch_shapes=[pltpu.VMEM((peers, out_lines, LANES), f32)],
        compiler_params=pltpu.CompilerParams(vmem_limit_bytes=8 * MIB),
        name="unpack",
    )(*looked)
    return jnp.transpose(result, (0, 2, 1))[None]


def packs(mesh, slc):
    peers = mesh.shape["line"]
    columns = slc.shape[2] // mesh.shape["stack"] // peers
    chunk_lines = slc.shape[3] // peers
    inner = slc.shape[3] // TAPS
    return (
        columns == HALF
        and all(peers == len(row) for row in EXCHANGE)
        and chunk_lines % (16 * TAPS) == 0
        and inner % LANES == 0
        and inner <= 4 * LANES
    )


def solution(mesh):
    specs = dict(
        mesh=mesh,
        in_specs=(P("date", None, "stack", "line"), P(), P()),
        out_specs=P("date", None, "stack", "line"),
        check_vma=False,
    )

    def whole(slc, band_start, band_stop):
        if not packs(mesh, slc):
            return jax.shard_map(general_shards, **specs)(slc, band_start, band_stop)
        step = jax.shard_map(packed_step, **specs)
        return step(slc, band_start, band_stop)

    return whole
```

profile of v0, /device:TPU:0, one launch (start us, length us, event | category | flops | bytes accessed | tf_op | source)
XLA Modules:
  0.0 36.1 jit_solution(5234549602457557426)
XLA Ops:
  0.0 0.0 copy-start.2
  0.0 1.1 %copy-done.2 = f32[1,2,256,320]{2,3,1,0:T(8,128)S(1)} copy-done((f32[1,2,256,320]{2,3,1,0:T(8,128)S(1)}, f32[1,2,256,320]{2,3,1,0:T(8,128)}, u32[]{:S(2)}) %copy-start.2) | copy-done | bytes 655384
  1.1 0.2 pack.1
  1.3 5.1 %collective-permute-start = (f32[320,128]{1,0:T(8,128)S(1)}, f32[320,128]{1,0:T(8,128)S(1)}, u32[]{:S(2)}, u32[]{:S(2)}) collective-permute-start(f32[320,128]{1,0:T(8,128)S(1)} %get-tuple-element.24), channel_id=1, source_target_pairs={{0,3},{1,2},{2,1},{3,0},{4,7},{5,6},{6,5},{7,4},{8,11},{9,10},{10,... | collective-permute-start | bytes 491528 | tf_op jit(solution)/shard_map/ppermute | solution.py:380
  6.5 0.0 collective-permute-start.1
  6.5 0.6 %collective-permute-start.2 = (f32[320,128]{1,0:T(8,128)S(1)}, f32[320,128]{1,0:T(8,128)S(1)}, u32[]{:S(2)}, u32[]{:S(2)}) collective-permute-start(f32[320,128]{1,0:T(8,128)S(1)} %get-tuple-element.26), channel_id=1, source_target_pairs={{0,2},{1,3},{2,0},{3,1},{4,6},{5,7},{6,4},{7,5},{8,10},{9,11},{10,... | collective-permute-start | bytes 491528 | tf_op jit(solution)/shard_map/ppermute | solution.py:380
  7.1 0.0 copy-start.4
  7.1 0.0 copy-start.5
  7.1 0.4 %collective-permute-start.3 = (f32[320,128]{1,0:T(8,128)S(1)}, f32[320,128]{1,0:T(8,128)S(1)}, u32[]{:S(2)}, u32[]{:S(2)}) collective-permute-start(f32[320,128]{1,0:T(8,128)S(1)} %get-tuple-element.23.refs_0_), channel_id=1, source_target_pairs={{0,12},{4,0},{8,4},{12,8},{1,13},{5,1},{9,5},{13,9},{2,14},{6,2},{... | collective-permute-start | bytes 491528 | tf_op jit(solution)/shard_map/ppermute | solution.py:27
  7.5 4.1 %collective-permute-done.refs_1_ = f32[320,128]{1,0:T(8,128)S(1)} collective-permute-done((f32[320,128]{1,0:T(8,128)S(1)}, f32[320,128]{1,0:T(8,128)S(1)}, u32[]{:S(2)}, u32[]{:S(2)}) %collective-permute-start) | collective-permute-done | bytes 163872 | tf_op jit(solution)/shard_map/ppermute | solution.py:380
  11.6 0.0 collective-permute-start.4
  11.6 3.7 %collective-permute-done.1.refs_2_ = f32[320,128]{1,0:T(8,128)S(1)} collective-permute-done((f32[320,128]{1,0:T(8,128)S(1)}, f32[320,128]{1,0:T(8,128)S(1)}, u32[]{:S(2)}, u32[]{:S(2)}) %collective-permute-start.1) | collective-permute-done | bytes 163872 | tf_op jit(solution)/shard_map/ppermute | solution.py:380
  15.2 1.0 %collective-permute-start.5 = (f32[320,128]{1,0:T(8,128)S(1)}, f32[320,128]{1,0:T(8,128)S(1)}, u32[]{:S(2)}, u32[]{:S(2)}) collective-permute-start(f32[320,128]{1,0:T(8,128)S(1)} %collective-permute-done.1.refs_2_), channel_id=1, source_target_pairs={{0,12},{4,0},{8,4},{12,8},{1,13},{5,1},{9,5},{13,9},{2,14},{6,2},{... | collective-permute-start | bytes 491528 | tf_op jit(solution)/shard_map/ppermute | solution.py:27
  16.2 4.1 %collective-permute-done.2.refs_3_ = f32[320,128]{1,0:T(8,128)S(1)} collective-permute-done((f32[320,128]{1,0:T(8,128)S(1)}, f32[320,128]{1,0:T(8,128)S(1)}, u32[]{:S(2)}, u32[]{:S(2)}) %collective-permute-start.2) | collective-permute-done | bytes 163872 | tf_op jit(solution)/shard_map/ppermute | solution.py:380
  20.4 0.3 collective-permute-start.6
  20.6 0.0 copy-start
  20.6 1.3 %copy-done = bf16[2,10,128,256]{3,2,1,0:T(8,128)(2,1)S(1)} copy-done((bf16[2,10,128,256]{3,2,1,0:T(8,128)(2,1)S(1)}, bf16[2,10,128,256]{3,2,1,0:T(8,128)(2,1)}, u32[]{:S(2)}) %copy-start) | copy-done | bytes 1310744
  21.9 0.0 copy-start.1
  21.9 1.3 %copy-done.1 = bf16[2,10,128,256]{3,2,1,0:T(8,128)(2,1)S(1)} copy-done((bf16[2,10,128,256]{3,2,1,0:T(8,128)(2,1)S(1)}, bf16[2,10,128,256]{3,2,1,0:T(8,128)(2,1)}, u32[]{:S(2)}) %copy-start.1) | copy-done | bytes 1310744
  23.3 0.0 copy-start.3
  23.3 1.1 %copy-done.3 = bf16[10,128,256]{2,1,0:T(8,128)(2,1)S(1)} copy-done((bf16[10,128,256]{2,1,0:T(8,128)(2,1)S(1)}, bf16[10,128,256]{2,1,0:T(8,128)(2,1)}, u32[]{:S(2)}) %copy-start.3) | copy-done | bytes 655384
  24.3 0.2 tables.1
  24.6 0.0 collective-permute-done.3.refs_4_
  24.6 0.0 collective-permute-done.4.refs_5_
  24.6 0.0 collective-permute-done.5.refs_6_
  24.6 0.0 copy-done.4
  24.6 0.0 copy-done.5
  24.6 2.8 %early.1 = (f32[10,128,128]{2,1,0:T(8,128)S(1)}, f32[10,128,128]{2,1,0:T(8,128)S(1)}, f32[10,128,128]{2,1,0:T(8,128)S(1)}, f32[10,128,128]{2,1,0:T(8,128)S(1)}) custom-call(s32[4]{0:T(128)S(1)} %copy-done.4, s32[4]{0:T(128)S(1)} %copy-done.5, bf16[2,10,128,256]{3,2,1,0:T(8,128)(2,1)S(1)} %get-tuple-element.22.ahead_ref, ...), custom_call_target="tpu_custom_call" | custom-call | tf_op jit(solution)/shard_map/early/pallas_call | solution.py:401
  27.4 0.0 collective-permute-done.6.sec_ref
  27.5 1.4 %late.1 = (f32[64,128]{1,0:T(8,128)S(1)}, f32[64,128]{1,0:T(8,128)S(1)}, f32[64,128]{1,0:T(8,128)S(1)}, f32[64,128]{1,0:T(8,128)S(1)}) custom-call(bf16[10,128,256]{2,1,0:T(8,128)(2,1)S(1)} %get-tuple-element.20.late_ref, bf16[2,10,128,256]{3,2,1,0:T(8,128)(2,1)S(1)} %get-tuple-element.21.back_ref, f32[10,128,128]{2,1,0:T(8,128)S(1)} %get-tuple-element.27.mid_ref, ...), custom_call_target="tpu_custom_call" | custom-call | tf_op jit(solution)/shard_map/late/pallas_call | solution.py:410
  28.9 0.1 collective-permute-start.7
  29.0 2.4 %collective-permute-start.8 = (f32[64,128]{1,0:T(8,128)S(1)}, f32[64,128]{1,0:T(8,128)S(1)}, u32[]{:S(2)}, u32[]{:S(2)}) collective-permute-start(f32[64,128]{1,0:T(8,128)S(1)} %get-tuple-element.33), channel_id=1, source_target_pairs={{0,3},{1,2},{2,1},{3,0},{4,7},{5,6},{6,5},{7,4},{8,11},{9,10},{10,... | collective-permute-start | bytes 98312 | tf_op jit(solution)/shard_map/ppermute | solution.py:380
  31.3 1.1 %collective-permute-start.9 = (f32[64,128]{1,0:T(8,128)S(1)}, f32[64,128]{1,0:T(8,128)S(1)}, u32[]{:S(2)}, u32[]{:S(2)}) collective-permute-start(f32[64,128]{1,0:T(8,128)S(1)} %get-tuple-element.34), channel_id=1, source_target_pairs={{0,1},{1,0},{2,3},{3,2},{4,5},{5,4},{6,7},{7,6},{8,9},{9,8},{10,11... | collective-permute-start | bytes 98312 | tf_op jit(solution)/shard_map/ppermute | solution.py:380
  32.4 2.4 %collective-permute-done.7.refs_1_ = f32[64,128]{1,0:T(8,128)S(1)} collective-permute-done((f32[64,128]{1,0:T(8,128)S(1)}, f32[64,128]{1,0:T(8,128)S(1)}, u32[]{:S(2)}, u32[]{:S(2)}) %collective-permute-start.7) | collective-permute-done | bytes 32800 | tf_op jit(solution)/shard_map/ppermute | solution.py:380
  34.8 0.0 collective-permute-done.8.refs_2_
  34.8 0.5 %collective-permute-done.9.refs_3_ = f32[64,128]{1,0:T(8,128)S(1)} collective-permute-done((f32[64,128]{1,0:T(8,128)S(1)}, f32[64,128]{1,0:T(8,128)S(1)}, u32[]{:S(2)}, u32[]{:S(2)}) %collective-permute-start.9) | collective-permute-done | bytes 32800 | tf_op jit(solution)/shard_map/ppermute | solution.py:380
  35.3 0.8 %unpack.1 = f32[2,64,256]{2,1,0:T(8,128)} custom-call(f32[64,128]{1,0:T(8,128)S(1)} %get-tuple-element.31.refs_0_, f32[64,128]{1,0:T(8,128)S(1)} %collective-permute-done.7.refs_1_, f32[64,128]{1,0:T(8,128)S(1)} %collective-permute-done.8.refs_2_, f32[64,128]{1,0:T(8,128)S(1)} %collective-permute-done.9.refs_3_), custom_call_target="tpu_custom_call" | custom-call | tf_op jit(solution)/shard_map/unpack/pallas_call | solution.py:427
Async XLA Ops:
  0.0 1.1 %copy-start.2 = (f32[1,2,256,320]{2,3,1,0:T(8,128)S(1)}, f32[1,2,256,320]{2,3,1,0:T(8,128)}, u32[]{:S(2)}) copy-start(f32[1,2,256,320]{2,3,1,0:T(8,128)} %param.6) | copy-start | bytes 1966084
  1.3 10.2 %collective-permute-start = (f32[320,128]{1,0:T(8,128)S(1)}, f32[320,128]{1,0:T(8,128)S(1)}, u32[]{:S(2)}, u32[]{:S(2)}) collective-permute-start(f32[320,128]{1,0:T(8,128)S(1)} %get-tuple-element.24), channel_id=1, source_target_pairs={{0,3},{1,2},{2,1},{3,0},{4,7},{5,6},{6,5},{7,4},{8,11},{9,10},{10,... | collective-permute-start | bytes 491528 | tf_op jit(solution)/shard_map/ppermute | solution.py:380
  6.5 8.8 %collective-permute-start.1 = (f32[320,128]{1,0:T(8,128)S(1)}, f32[320,128]{1,0:T(8,128)S(1)}, u32[]{:S(2)}, u32[]{:S(2)}) collective-permute-start(f32[320,128]{1,0:T(8,128)S(1)} %get-tuple-element.25), channel_id=1, source_target_pairs={{0,1},{1,0},{2,3},{3,2},{4,5},{5,4},{6,7},{7,6},{8,9},{9,8},{10,11... | collective-permute-start | bytes 491528 | tf_op jit(solution)/shard_map/ppermute | solution.py:380
  6.5 13.9 %collective-permute-start.2 = (f32[320,128]{1,0:T(8,128)S(1)}, f32[320,128]{1,0:T(8,128)S(1)}, u32[]{:S(2)}, u32[]{:S(2)}) collective-permute-start(f32[320,128]{1,0:T(8,128)S(1)} %get-tuple-element.26), channel_id=1, source_target_pairs={{0,2},{1,3},{2,0},{3,1},{4,6},{5,7},{6,4},{7,5},{8,10},{9,11},{10,... | collective-permute-start | bytes 491528 | tf_op jit(solution)/shard_map/ppermute | solution.py:380
  7.1 17.5 %copy-start.4 = (s32[4]{0:T(128)S(1)}, s32[4]{0:T(128)}, u32[]{:S(2)}) copy-start(s32[4]{0:T(128)} %start_ref.1) | copy-start | bytes 52
  7.1 17.5 %copy-start.5 = (s32[4]{0:T(128)S(1)}, s32[4]{0:T(128)}, u32[]{:S(2)}) copy-start(s32[4]{0:T(128)} %stop_ref.1) | copy-start | bytes 52
  7.1 17.4 %collective-permute-start.3 = (f32[320,128]{1,0:T(8,128)S(1)}, f32[320,128]{1,0:T(8,128)S(1)}, u32[]{:S(2)}, u32[]{:S(2)}) collective-permute-start(f32[320,128]{1,0:T(8,128)S(1)} %get-tuple-element.23.refs_0_), channel_id=1, source_target_pairs={{0,12},{4,0},{8,4},{12,8},{1,13},{5,1},{9,5},{13,9},{2,14},{6,2},{... | collective-permute-start | bytes 491528 | tf_op jit(solution)/shard_map/ppermute | solution.py:27
  11.6 13.0 %collective-permute-start.4 = (f32[320,128]{1,0:T(8,128)S(1)}, f32[320,128]{1,0:T(8,128)S(1)}, u32[]{:S(2)}, u32[]{:S(2)}) collective-permute-start(f32[320,128]{1,0:T(8,128)S(1)} %collective-permute-done.refs_1_), channel_id=1, source_target_pairs={{0,12},{4,0},{8,4},{12,8},{1,13},{5,1},{9,5},{13,9},{2,14},{6,2},{... | collective-permute-start | bytes 491528 | tf_op jit(solution)/shard_map/ppermute | solution.py:27
  15.2 9.3 %collective-permute-start.5 = (f32[320,128]{1,0:T(8,128)S(1)}, f32[320,128]{1,0:T(8,128)S(1)}, u32[]{:S(2)}, u32[]{:S(2)}) collective-permute-start(f32[320,128]{1,0:T(8,128)S(1)} %collective-permute-done.1.refs_2_), channel_id=1, source_target_pairs={{0,12},{4,0},{8,4},{12,8},{1,13},{5,1},{9,5},{13,9},{2,14},{6,2},{... | collective-permute-start | bytes 491528 | tf_op jit(solution)/shard_map/ppermute | solution.py:27
  20.4 7.1 %collective-permute-start.6 = (f32[320,128]{1,0:T(8,128)S(1)}, f32[320,128]{1,0:T(8,128)S(1)}, u32[]{:S(2)}, u32[]{:S(2)}) collective-permute-start(f32[320,128]{1,0:T(8,128)S(1)} %collective-permute-done.2.refs_3_), channel_id=1, source_target_pairs={{0,12},{4,0},{8,4},{12,8},{1,13},{5,1},{9,5},{13,9},{2,14},{6,2},{... | collective-permute-start | bytes 491528 | tf_op jit(solution)/shard_map/ppermute | solution.py:27
  20.6 1.3 %copy-start = (bf16[2,10,128,256]{3,2,1,0:T(8,128)(2,1)S(1)}, bf16[2,10,128,256]{3,2,1,0:T(8,128)(2,1)}, u32[]{:S(2)}) copy-start(bf16[2,10,128,256]{3,2,1,0:T(8,128)(2,1)} %constant.6.clone.refs_0_) | copy-start | bytes 3932164
  21.9 1.3 %copy-start.1 = (bf16[2,10,128,256]{3,2,1,0:T(8,128)(2,1)S(1)}, bf16[2,10,128,256]{3,2,1,0:T(8,128)(2,1)}, u32[]{:S(2)}) copy-start(bf16[2,10,128,256]{3,2,1,0:T(8,128)(2,1)} %constant.7.clone.refs_1_) | copy-start | bytes 3932164
  23.3 1.1 %copy-start.3 = (bf16[10,128,256]{2,1,0:T(8,128)(2,1)S(1)}, bf16[10,128,256]{2,1,0:T(8,128)(2,1)}, u32[]{:S(2)}) copy-start(bf16[10,128,256]{2,1,0:T(8,128)(2,1)} %constant.8.clone.refs_2_) | copy-start | bytes 1966084
  28.9 5.9 %collective-permute-start.7 = (f32[64,128]{1,0:T(8,128)S(1)}, f32[64,128]{1,0:T(8,128)S(1)}, u32[]{:S(2)}, u32[]{:S(2)}) collective-permute-start(f32[64,128]{1,0:T(8,128)S(1)} %get-tuple-element.32), channel_id=1, source_target_pairs={{0,2},{1,3},{2,0},{3,1},{4,6},{5,7},{6,4},{7,5},{8,10},{9,11},{10,... | collective-permute-start | bytes 98312 | tf_op jit(solution)/shard_map/ppermute | solution.py:380
  29.0 5.9 %collective-permute-start.8 = (f32[64,128]{1,0:T(8,128)S(1)}, f32[64,128]{1,0:T(8,128)S(1)}, u32[]{:S(2)}, u32[]{:S(2)}) collective-permute-start(f32[64,128]{1,0:T(8,128)S(1)} %get-tuple-element.33), channel_id=1, source_target_pairs={{0,3},{1,2},{2,1},{3,0},{4,7},{5,6},{6,5},{7,4},{8,11},{9,10},{10,... | collective-permute-start | bytes 98312 | tf_op jit(solution)/shard_map/ppermute | solution.py:380
  31.3 4.0 %collective-permute-start.9 = (f32[64,128]{1,0:T(8,128)S(1)}, f32[64,128]{1,0:T(8,128)S(1)}, u32[]{:S(2)}, u32[]{:S(2)}) collective-permute-start(f32[64,128]{1,0:T(8,128)S(1)} %get-tuple-element.34), channel_id=1, source_target_pairs={{0,1},{1,0},{2,3},{3,2},{4,5},{5,4},{6,7},{7,6},{8,9},{9,8},{10,11... | collective-permute-start | bytes 98312 | tf_op jit(solution)/shard_map/ppermute | solution.py:380
where the time goes:
time: 36.4 us; the launch traced here: 36.1 us
  waiting for transfers between devices  14.8 us (41%)
  starting transfers between devices  11 us (30%)
  Pallas kernels  5.48 us (15%)
  local copies, waits for them, and re-layouts  4.81 us (13%)
    ppermute x6, waiting for transfers between devices, exchange(): return lax.ppermute(values, 'line', list(enumerate(row)))  14.8 us
    ppermute x6, starting transfers between devices, exchange(): return lax.ppermute(values, 'line', list(enumerate(row)))  9.33 us
    unnamed x12, local copies, waits for them, and re-layouts  4.81 us
    pallas_call x1, Pallas kernels, packed_step(): pl.pallas_call(functools.partial(early_kernel, peers), out_shape=[taps] *...  2.82 us
    ppermute x4, starting transfers between devices, shifted(): lax.ppermute(shard, axis, [(i, (i + by) % size) for i in range(size)])  1.63 us
    pallas_call x1, Pallas kernels, packed_step(): pl.pallas_call(functools.partial(late_kernel, peers), out_shape=[jax.Shap...  1.43 us
    pallas_call x1, Pallas kernels, packed_step(): pl.pallas_call(functools.partial(unpack_kernel, peers), out_shape=jax.Sha...  0.77 us
  transfers between devices with their start and end apart: 10, of which 5 were waited for; matrix products, arithmetic and copies ran while one was open for 0% of the time, Pallas kernels for 8%

commit v1 on v0

--- a/solution.py
+++ b/solution.py
@@ -188,14 +188,20 @@
 
 def pack_kernel(image_ref, *chunk_refs):
     me = lax.axis_index("line")
-    for row, chunk_ref in zip((None,) + EXCHANGE, chunk_refs):
-        block = me if row is None else entry(row, me)
+    peers = len(chunk_refs) - 1
+    for q in range(peers):
+        block = entry(EXCHANGE[q - 1], me) if q else me
         lane = pl.multiple_of(block // 2 * LANES, LANES)
         side = block % 2
         stay = image_ref[side, :, pl.ds(lane, LANES)]
         move = image_ref[1 - side, :, pl.ds(lane, LANES)]
         half = lax.broadcasted_iota(jnp.int32, stay.shape, 1) // HALF
-        chunk_ref[...] = jnp.where(half == side, stay, swap_halves(move))
+        value = jnp.where(half == side, stay, swap_halves(move))
+        if q < peers - 1:
+            chunk_refs[q][...] = value
+        else:
+            cut = value.shape[0] // 2
+            chunk_refs[q][...], chunk_refs[q + 1][...] = value[:cut], value[cut:]
 
 
 COS1, COS2 = math.cos(2.0 * math.pi / 5), math.cos(4.0 * math.pi / 5)
@@ -265,19 +271,28 @@
         target[...] = source[...]
 
 
-def early_kernel(peers, start_ref, stop_ref, ahead_ref, back_ref, *refs):
-    own_refs, sec_refs = refs[:peers], refs[peers : 2 * peers - 1]
-    mid_ref, weight_ref, same_ref, cross_ref = refs[2 * peers - 1 : 2 * peers + 3]
+def weights_kernel(start_ref, stop_ref, weight_ref):
+    taps, inner = weight_ref.shape[:2]
+    date = lax.axis_index("date")
+    start, stop = start_ref[date], stop_ref[date]
+    for m in range(taps):
+        bin_index = lax.broadcasted_iota(jnp.int32, (inner, LANES), 0) + m * inner
+        keep = (bin_index >= start) & (bin_index < stop)
+        weight_ref[m] = jnp.where(keep, 1.0 / (taps * inner), 0.0)
+
+
+def early_kernel(peers, ahead_ref, back_ref, weight_ref, *refs):
+    own_refs, sec_refs = refs[: peers + 1], refs[peers + 1 : 2 * peers]
+    mid_ref, same_ref, cross_ref = refs[2 * peers : 2 * peers + 3]
     own_ref, own_turned_ref, sec_ref, sec_turned_ref = refs[2 * peers + 3 : -2]
     own_mid_ref, own_back_ref = refs[-2:]
     me = lax.axis_index("line")
-    date = lax.axis_index("date")
     lines = own_ref.shape[0] // peers
     inner = own_ref.shape[0] // TAPS
     for q in range(peers):
         block = entry(senders(EXCHANGE[q - 1]), me) if q else me
         span = pl.ds(pl.multiple_of(block_of(me, block, peers) * lines, 8), lines)
-        own = own_refs[q][...]
+        own = own_refs[q][...] if q < peers - 1 else stacked(own_refs[q][...], own_refs[q + 1][...])
         own_ref[span, :] = own
         own_turned_ref[span, :] = turned(own)
         if q == peers - 1:
@@ -300,11 +315,6 @@
         own_mid_ref[l] = bins[:, :LANES]
         mid_ref[l] = bins[:, LANES:]
 
-    first, stop = start_ref[date], stop_ref[date]
-    for m in range(TAPS):
-        bin_index = lax.broadcasted_iota(jnp.int32, (inner, LANES), 0) + m * inner
-        keep = (bin_index >= first) & (bin_index < stop)
-        weight_ref[m] = jnp.where(keep, 1.0 / (TAPS * inner), 0.0)
     spectral(own_mid_ref, weight_ref, own_back_ref)
     for l in range(TAPS):
         signal = signal_of(own_back_ref, back_ref, l) * (1.0 / LOOKS)
@@ -315,17 +325,17 @@
 
 
 def late_kernel(
-    peers, late_ref, back_ref, mid_ref, weight_ref, same_ref, cross_ref, sec_ref, *refs
+    peers, late_ref, back_ref, mid_ref, weight_ref, same_ref, cross_ref, sec_ref, rest_ref, *refs
 ):
     out_refs = refs[:peers]
     total_ref, taps_ref, sum_ref = refs[peers:]
     me = lax.axis_index("line")
     inner = mid_ref.shape[1]
-    few = sec_ref.shape[0] // TAPS
+    few = 2 * sec_ref.shape[0] // TAPS
     rest = jnp.zeros((late_ref.shape[2] - 6 * few, LANES), jnp.bfloat16)
     for l in range(TAPS):
-        span = pl.ds(l, few, stride=TAPS)
-        values = sec_ref[span, :]
+        span = pl.ds(l, few // 2, stride=TAPS)
+        values = stacked(sec_ref[span, :], rest_ref[span, :])
         high, low = split_pair(stacked(values, turned(values)))
         total_ref[l] = mid_ref[l] + product(late_ref[l], stacked(high, low, high, rest))
     spectral(total_ref, weight_ref, taps_ref)
@@ -367,11 +377,13 @@
     smem = pl.BlockSpec(memory_space=pltpu.SMEM)
     params = pltpu.CompilerParams(vmem_limit_bytes=16 * MIB)
     image = jnp.transpose(slc[0], (0, 2, 1))
+    chunk = jax.ShapeDtypeStruct((chunk_lines, LANES), f32)
+    part = jax.ShapeDtypeStruct((chunk_lines // 2, LANES), f32)
     packed = pl.pallas_call(
         pack_kernel,
-        out_shape=[jax.ShapeDtypeStruct((chunk_lines, LANES), f32)] * peers,
+        out_shape=[chunk] * (peers - 1) + [part] * 2,
         in_specs=[vmem],
-        out_specs=[vmem] * peers,
+        out_specs=[vmem] * (peers + 1),
         compiler_params=pltpu.CompilerParams(vmem_limit_bytes=8 * MIB),
         name="pack",
     )(image)
@@ -383,11 +395,12 @@
         return shifted(values, "date", -1)
 
     own = [
-        exchange(values, EXCHANGE[q - 1]) if q else values
+        exchange(values, EXCHANGE[min(q, peers - 1) - 1]) if q else values
         for q, values in enumerate(packed)
     ]
     sec = [forward(values) for values in own]
     tables = [jnp.asarray(table) for table in host_tables(inner, 0, chunk_lines // TAPS)]
+    taps = jax.ShapeDtypeStruct((TAPS, inner, LANES), f32)
     ahead_table, back_table, late_table = pl.pallas_call(
         functools.partial(tables_kernel, len(tables)),
         out_shape=[jax.ShapeDtypeStruct(table.shape, table.dtype) for table in tables],
@@ -396,21 +409,28 @@
         compiler_params=params,
         name="tables",
     )(*tables)
-    taps = jax.ShapeDtypeStruct((TAPS, inner, LANES), f32)
+    weight = pl.pallas_call(
+        weights_kernel,
+        out_shape=taps,
+        in_specs=[smem, smem],
+        out_specs=vmem,
+        compiler_params=params,
+        name="weights",
+    )(band_start, band_stop)
     plane = pltpu.VMEM((peers * chunk_lines, LANES), f32)
-    middle, weight, same, cross = pl.pallas_call(
+    middle, same, cross = pl.pallas_call(
         functools.partial(early_kernel, peers),
-        out_shape=[taps] * 4,
-        in_specs=[smem, smem] + [vmem] * (2 * peers + 1),
-        out_specs=[vmem] * 4,
+        out_shape=[taps] * 3,
+        in_specs=[vmem] * (2 * peers + 3),
+        out_specs=[vmem] * 3,
         scratch_shapes=[plane] * 4 + [pltpu.VMEM(taps.shape, f32)] * 2,
         compiler_params=params,
         name="early",
-    )(band_start, band_stop, ahead_table, back_table, *own, *sec[:-1])
+    )(ahead_table, back_table, weight, *own, *sec[:-2])
     looked = pl.pallas_call(
         functools.partial(late_kernel, peers),
         out_shape=[jax.ShapeDtypeStruct((out_lines, LANES), f32)] * peers,
-        in_specs=[vmem] * 7,
+        in_specs=[vmem] * 8,
         out_specs=[vmem] * peers,
         scratch_shapes=[
             pltpu.VMEM(taps.shape, f32),
@@ -419,11 +439,8 @@
         ],
         compiler_params=params,
         name="late",
-    )(late_table, back_table, middle, weight, same, cross, sec[-1])
-    looked = [
-        exchange(values, RETURN[q - 1]) if q else values
-        for q, values in enumerate(looked)
-    ]
+    )(late_table, back_table, middle, weight, same, cross, *sec[-2:])
+    looked = [exchange(values, RETURN[q - 1]) if q else values for q, values in enumerate(looked)]
     result = pl.pallas_call(
         functools.partial(unpack_kernel, peers),
         out_shape=jax.ShapeDtypeStruct((2, out_lines, slc.shape[2]), f32),
@@ -444,7 +461,7 @@
     return (
         columns == HALF
         and all(peers == len(row) for row in EXCHANGE)
-        and chunk_lines % (16 * TAPS) == 0
+        and chunk_lines % (32 * TAPS) == 0
         and inner % LANES == 0
         and inner <= 4 * LANES
     )

time: 36.4 us -> 41.5 us (1.14)
  starting transfers between devices: 11 us -> 14 us
  waiting for transfers between devices: 14.8 us -> 16.8 us
    ppermute x6 -> x7, starting transfers between devices: 9.33 us -> 11.6 us  [exchange(): return lax.ppermute(values, 'line', list(enumerate(row)))]
    ppermute x6 -> x7, waiting for transfers between devices: 14.8 us -> 16.8 us  [exchange(): return lax.ppermute(values, 'line', list(enumerate(row)))]
    ppermute x4 -> x5, starting transfers between devices: 1.63 us -> 2.34 us  [shifted(): lax.ppermute(shard, axis, [(i, (i + by) % size) for i in range(size)])]
    pallas_call x1 -> x2, Pallas kernels: 0.24 us -> 0.9 us  [the longest x1 0.67 us: packed_step(): pl.pallas_call(weights_kernel, out_shape=taps, in_specs=[smem, smem], out...]
    pallas_call x1, Pallas kernels: 2.82 us -> 2.19 us  [packed_step(): pl.pallas_call(functools.partial(early_kernel, peers), out_shape=[taps] *...]
  transfers between devices with their start and end apart: 10 -> 12, of which waited for: 5 -> 7; matrix products, arithmetic and copies ran while one was open for 0% -> 0% of each run, Pallas kernels for 8% -> 7%
where the time goes in v1:
time: 41.5 us; the launch traced here: 41.3 us
  waiting for transfers between devices  16.8 us (40%)
  starting transfers between devices  14 us (34%)
  Pallas kernels  5.5 us (13%)
  local copies, waits for them, and re-layouts  4.9 us (12%)
    ppermute x7, waiting for transfers between devices, exchange(): return lax.ppermute(values, 'line', list(enumerate(row)))  16.8 us
    ppermute x7, starting transfers between devices, exchange(): return lax.ppermute(values, 'line', list(enumerate(row)))  11.6 us
    unnamed x12, local copies, waits for them, and re-layouts  4.9 us
    ppermute x5, starting transfers between devices, shifted(): lax.ppermute(shard, axis, [(i, (i + by) % size) for i in range(size)])  2.34 us
    pallas_call x1, Pallas kernels, packed_step(): pl.pallas_call(functools.partial(early_kernel, peers), out_shape=[taps] *...  2.19 us
    pallas_call x1, Pallas kernels, packed_step(): pl.pallas_call(functools.partial(late_kernel, peers), out_shape=[jax.Shap...  1.42 us
  transfers between devices with their start and end apart: 12, of which 7 were waited for; matrix products, arithmetic and copies ran while one was open for 0% of the time, Pallas kernels for 7%

profile of v1, /device:TPU:0, one launch (start us, length us, event | category | flops | bytes accessed | tf_op | source)
XLA Modules:
  0.0 41.3 jit_solution(11788258801477350520)
XLA Ops:
  0.0 0.0 copy-start
  0.0 0.0 copy-start.2
  0.0 1.2 %copy-done.2 = f32[1,2,256,320]{2,3,1,0:T(8,128)S(1)} copy-done((f32[1,2,256,320]{2,3,1,0:T(8,128)S(1)}, f32[1,2,256,320]{2,3,1,0:T(8,128)}, u32[]{:S(2)}) %copy-start.2) | copy-done | bytes 655384
  1.2 0.2 pack.1
  1.4 5.1 %collective-permute-start = (f32[320,128]{1,0:T(8,128)S(1)}, f32[320,128]{1,0:T(8,128)S(1)}, u32[]{:S(2)}, u32[]{:S(2)}) collective-permute-start(f32[320,128]{1,0:T(8,128)S(1)} %get-tuple-element.24), channel_id=1, source_target_pairs={{0,3},{1,2},{2,1},{3,0},{4,7},{5,6},{6,5},{7,4},{8,11},{9,10},{10,... | collective-permute-start | bytes 491528 | tf_op jit(solution)/shard_map/ppermute | solution.py:392
  6.6 0.0 collective-permute-start.1
  6.6 0.7 %collective-permute-start.4 = (f32[320,128]{1,0:T(8,128)S(1)}, f32[320,128]{1,0:T(8,128)S(1)}, u32[]{:S(2)}, u32[]{:S(2)}) collective-permute-start(f32[320,128]{1,0:T(8,128)S(1)} %get-tuple-element.23.refs_0_), channel_id=1, source_target_pairs={{0,12},{4,0},{8,4},{12,8},{1,13},{5,1},{9,5},{13,9},{2,14},{6,2},{... | collective-permute-start | bytes 491528 | tf_op jit(solution)/shard_map/ppermute | solution.py:27
  7.2 4.4 %collective-permute-done.refs_1_ = f32[320,128]{1,0:T(8,128)S(1)} collective-permute-done((f32[320,128]{1,0:T(8,128)S(1)}, f32[320,128]{1,0:T(8,128)S(1)}, u32[]{:S(2)}, u32[]{:S(2)}) %collective-permute-start) | collective-permute-done | bytes 163872 | tf_op jit(solution)/shard_map/ppermute | solution.py:392
  11.7 0.0 collective-permute-start.5
  11.7 2.7 %collective-permute-done.1.refs_2_ = f32[320,128]{1,0:T(8,128)S(1)} collective-permute-done((f32[320,128]{1,0:T(8,128)S(1)}, f32[320,128]{1,0:T(8,128)S(1)}, u32[]{:S(2)}, u32[]{:S(2)}) %collective-permute-start.1) | collective-permute-done | bytes 163872 | tf_op jit(solution)/shard_map/ppermute | solution.py:392
  14.4 1.1 %collective-permute-start.6 = (f32[320,128]{1,0:T(8,128)S(1)}, f32[320,128]{1,0:T(8,128)S(1)}, u32[]{:S(2)}, u32[]{:S(2)}) collective-permute-start(f32[320,128]{1,0:T(8,128)S(1)} %collective-permute-done.1.refs_2_), channel_id=1, source_target_pairs={{0,12},{4,0},{8,4},{12,8},{1,13},{5,1},{9,5},{13,9},{2,14},{6,2},{... | collective-permute-start | bytes 491528 | tf_op jit(solution)/shard_map/ppermute | solution.py:27
  15.5 1.1 %collective-permute-start.2 = (f32[160,128]{1,0:T(8,128)S(1)}, f32[160,128]{1,0:T(8,128)S(1)}, u32[]{:S(2)}, u32[]{:S(2)}) collective-permute-start(f32[160,128]{1,0:T(8,128)S(1)} %get-tuple-element.26), channel_id=1, source_target_pairs={{0,2},{1,3},{2,0},{3,1},{4,6},{5,7},{6,4},{7,5},{8,10},{9,11},{10,... | collective-permute-start | bytes 245768 | tf_op jit(solution)/shard_map/ppermute | solution.py:392
  16.6 1.8 %collective-permute-start.3 = (f32[160,128]{1,0:T(8,128)S(1)}, f32[160,128]{1,0:T(8,128)S(1)}, u32[]{:S(2)}, u32[]{:S(2)}) collective-permute-start(f32[160,128]{1,0:T(8,128)S(1)} %get-tuple-element.27), channel_id=1, source_target_pairs={{0,2},{1,3},{2,0},{3,1},{4,6},{5,7},{6,4},{7,5},{8,10},{9,11},{10,... | collective-permute-start | bytes 245768 | tf_op jit(solution)/shard_map/ppermute | solution.py:392
  18.4 6.1 %collective-permute-done.2.refs_3_ = f32[160,128]{1,0:T(8,128)S(1)} collective-permute-done((f32[160,128]{1,0:T(8,128)S(1)}, f32[160,128]{1,0:T(8,128)S(1)}, u32[]{:S(2)}, u32[]{:S(2)}) %collective-permute-start.2) | collective-permute-done | bytes 81952 | tf_op jit(solution)/shard_map/ppermute | solution.py:392
  24.5 0.0 collective-permute-start.7
  24.5 0.9 %collective-permute-done.3.refs_4_ = f32[160,128]{1,0:T(8,128)S(1)} collective-permute-done((f32[160,128]{1,0:T(8,128)S(1)}, f32[160,128]{1,0:T(8,128)S(1)}, u32[]{:S(2)}, u32[]{:S(2)}) %collective-permute-start.3) | collective-permute-done | bytes 81952 | tf_op jit(solution)/shard_map/ppermute | solution.py:392
  25.4 0.6 %collective-permute-start.8 = (f32[160,128]{1,0:T(8,128)S(1)}, f32[160,128]{1,0:T(8,128)S(1)}, u32[]{:S(2)}, u32[]{:S(2)}) collective-permute-start(f32[160,128]{1,0:T(8,128)S(1)} %collective-permute-done.3.refs_4_), channel_id=1, source_target_pairs={{0,12},{4,0},{8,4},{12,8},{1,13},{5,1},{9,5},{13,9},{2,14},{6,2},{... | collective-permute-start | bytes 245768 | tf_op jit(solution)/shard_map/ppermute | solution.py:27
  26.0 0.0 copy-start.4
  26.0 0.7 %copy-done.4 = s32[4]{0:T(128)S(1)} copy-done((s32[4]{0:T(128)S(1)}, s32[4]{0:T(128)}, u32[]{:S(2)}) %copy-start.4) | copy-done | bytes 40
  26.7 0.0 copy-start.5
  26.7 0.7 %copy-done.5 = s32[4]{0:T(128)S(1)} copy-done((s32[4]{0:T(128)S(1)}, s32[4]{0:T(128)}, u32[]{:S(2)}) %copy-start.5) | copy-done | bytes 40
  27.3 0.7 %weights.1.weight_ref = f32[10,128,128]{2,1,0:T(8,128)S(1)} custom-call(s32[4]{0:T(128)S(1)} %copy-done.4, s32[4]{0:T(128)S(1)} %copy-done.5), custom_call_target="tpu_custom_call" | custom-call | tf_op jit(solution)/shard_map/weights/pallas_call | solution.py:412
  28.0 0.0 copy-done
  28.0 0.0 copy-start.1
  28.0 1.3 %copy-done.1 = bf16[2,10,128,256]{3,2,1,0:T(8,128)(2,1)S(1)} copy-done((bf16[2,10,128,256]{3,2,1,0:T(8,128)(2,1)S(1)}, bf16[2,10,128,256]{3,2,1,0:T(8,128)(2,1)}, u32[]{:S(2)}) %copy-start.1) | copy-done | bytes 1310744
  29.3 0.0 copy-start.3
  29.3 1.1 %copy-done.3 = bf16[10,128,256]{2,1,0:T(8,128)(2,1)S(1)} copy-done((bf16[10,128,256]{2,1,0:T(8,128)(2,1)S(1)}, bf16[10,128,256]{2,1,0:T(8,128)(2,1)}, u32[]{:S(2)}) %copy-start.3) | copy-done | bytes 655384
  30.4 0.2 tables.1
  30.6 0.0 collective-permute-done.4.refs_5_
  30.6 0.0 collective-permute-done.5.refs_6_
  30.7 0.0 collective-permute-done.6.refs_7_
  30.7 2.2 %early.1 = (f32[10,128,128]{2,1,0:T(8,128)S(1)}, f32[10,128,128]{2,1,0:T(8,128)S(1)}, f32[10,128,128]{2,1,0:T(8,128)S(1)}) custom-call(bf16[2,10,128,256]{3,2,1,0:T(8,128)(2,1)S(1)} %get-tuple-element.22.ahead_ref, bf16[2,10,128,256]{3,2,1,0:T(8,128)(2,1)S(1)} %get-tuple-element.21.back_ref, f32[10,128,128]{2,1,0:T(8,128)S(1)} %weights.1.weight_ref, ...), custom_call_target="tpu_custom_call" | custom-call | tf_op jit(solution)/shard_map/early/pallas_call | solution.py:421
  32.9 0.0 collective-permute-done.7.sec_ref
  32.9 0.0 collective-permute-done.8.rest_ref
  32.9 1.4 %late.1 = (f32[64,128]{1,0:T(8,128)S(1)}, f32[64,128]{1,0:T(8,128)S(1)}, f32[64,128]{1,0:T(8,128)S(1)}, f32[64,128]{1,0:T(8,128)S(1)}) custom-call(bf16[10,128,256]{2,1,0:T(8,128)(2,1)S(1)} %get-tuple-element.20.late_ref, bf16[2,10,128,256]{3,2,1,0:T(8,128)(2,1)S(1)} %get-tuple-element.21.back_ref, f32[10,128,128]{2,1,0:T(8,128)S(1)} %get-tuple-element.28.mid_ref, ...), custom_call_target="tpu_custom_call" | custom-call | tf_op jit(solution)/shard_map/late/pallas_call | solution.py:430
  34.3 0.1 collective-permute-start.9
  34.4 2.2 %collective-permute-start.10 = (f32[64,128]{1,0:T(8,128)S(1)}, f32[64,128]{1,0:T(8,128)S(1)}, u32[]{:S(2)}, u32[]{:S(2)}) collective-permute-start(f32[64,128]{1,0:T(8,128)S(1)} %get-tuple-element.33), channel_id=1, source_target_pairs={{0,3},{1,2},{2,1},{3,0},{4,7},{5,6},{6,5},{7,4},{8,11},{9,10},{10,... | collective-permute-start | bytes 98312 | tf_op jit(solution)/shard_map/ppermute | solution.py:392
  36.6 1.3 %collective-permute-start.11 = (f32[64,128]{1,0:T(8,128)S(1)}, f32[64,128]{1,0:T(8,128)S(1)}, u32[]{:S(2)}, u32[]{:S(2)}) collective-permute-start(f32[64,128]{1,0:T(8,128)S(1)} %get-tuple-element.34), channel_id=1, source_target_pairs={{0,1},{1,0},{2,3},{3,2},{4,5},{5,4},{6,7},{7,6},{8,9},{9,8},{10,11... | collective-permute-start | bytes 98312 | tf_op jit(solution)/shard_map/ppermute | solution.py:392
  37.9 1.7 %collective-permute-done.9.refs_1_ = f32[64,128]{1,0:T(8,128)S(1)} collective-permute-done((f32[64,128]{1,0:T(8,128)S(1)}, f32[64,128]{1,0:T(8,128)S(1)}, u32[]{:S(2)}, u32[]{:S(2)}) %collective-permute-start.9) | collective-permute-done | bytes 32800 | tf_op jit(solution)/shard_map/ppermute | solution.py:392
  39.5 0.6 %collective-permute-done.10.refs_2_ = f32[64,128]{1,0:T(8,128)S(1)} collective-permute-done((f32[64,128]{1,0:T(8,128)S(1)}, f32[64,128]{1,0:T(8,128)S(1)}, u32[]{:S(2)}, u32[]{:S(2)}) %collective-permute-start.10) | collective-permute-done | bytes 32800 | tf_op jit(solution)/shard_map/ppermute | solution.py:392
  40.2 0.3 collective-permute-done.11.refs_3_
  40.5 0.8 %unpack.1 = f32[2,64,256]{2,1,0:T(8,128)} custom-call(f32[64,128]{1,0:T(8,128)S(1)} %get-tuple-element.31.refs_0_, f32[64,128]{1,0:T(8,128)S(1)} %collective-permute-done.9.refs_1_, f32[64,128]{1,0:T(8,128)S(1)} %collective-permute-done.10.refs_2_, f32[64,128]{1,0:T(8,128)S(1)} %collective-permute-done.11.refs_3_), custom_call_target="tpu_custom_call" | custom-call | tf_op jit(solution)/shard_map/unpack/pallas_call | solution.py:444
Async XLA Ops:
  0.0 28.0 %copy-start = (bf16[2,10,128,256]{3,2,1,0:T(8,128)(2,1)S(1)}, bf16[2,10,128,256]{3,2,1,0:T(8,128)(2,1)}, u32[]{:S(2)}) copy-start(bf16[2,10,128,256]{3,2,1,0:T(8,128)(2,1)} %constant.6.clone.refs_0_) | copy-start | bytes 3932164
  0.0 1.2 %copy-start.2 = (f32[1,2,256,320]{2,3,1,0:T(8,128)S(1)}, f32[1,2,256,320]{2,3,1,0:T(8,128)}, u32[]{:S(2)}) copy-start(f32[1,2,256,320]{2,3,1,0:T(8,128)} %param.6) | copy-start | bytes 1966084
  1.4 10.2 %collective-permute-start = (f32[320,128]{1,0:T(8,128)S(1)}, f32[320,128]{1,0:T(8,128)S(1)}, u32[]{:S(2)}, u32[]{:S(2)}) collective-permute-start(f32[320,128]{1,0:T(8,128)S(1)} %get-tuple-element.24), channel_id=1, source_target_pairs={{0,3},{1,2},{2,1},{3,0},{4,7},{5,6},{6,5},{7,4},{8,11},{9,10},{10,... | collective-permute-start | bytes 491528 | tf_op jit(solution)/shard_map/ppermute | solution.py:392
  6.6 7.8 %collective-permute-start.1 = (f32[320,128]{1,0:T(8,128)S(1)}, f32[320,128]{1,0:T(8,128)S(1)}, u32[]{:S(2)}, u32[]{:S(2)}) collective-permute-start(f32[320,128]{1,0:T(8,128)S(1)} %get-tuple-element.25), channel_id=1, source_target_pairs={{0,1},{1,0},{2,3},{3,2},{4,5},{5,4},{6,7},{7,6},{8,9},{9,8},{10,11... | collective-permute-start | bytes 491528 | tf_op jit(solution)/shard_map/ppermute | solution.py:392
  6.6 24.0 %collective-permute-start.4 = (f32[320,128]{1,0:T(8,128)S(1)}, f32[320,128]{1,0:T(8,128)S(1)}, u32[]{:S(2)}, u32[]{:S(2)}) collective-permute-start(f32[320,128]{1,0:T(8,128)S(1)} %get-tuple-element.23.refs_0_), channel_id=1, source_target_pairs={{0,12},{4,0},{8,4},{12,8},{1,13},{5,1},{9,5},{13,9},{2,14},{6,2},{... | collective-permute-start | bytes 491528 | tf_op jit(solution)/shard_map/ppermute | solution.py:27
  11.7 19.0 %collective-permute-start.5 = (f32[320,128]{1,0:T(8,128)S(1)}, f32[320,128]{1,0:T(8,128)S(1)}, u32[]{:S(2)}, u32[]{:S(2)}) collective-permute-start(f32[320,128]{1,0:T(8,128)S(1)} %collective-permute-done.refs_1_), channel_id=1, source_target_pairs={{0,12},{4,0},{8,4},{12,8},{1,13},{5,1},{9,5},{13,9},{2,14},{6,2},{... | collective-permute-start | bytes 491528 | tf_op jit(solution)/shard_map/ppermute | solution.py:27
  14.4 16.3 %collective-permute-start.6 = (f32[320,128]{1,0:T(8,128)S(1)}, f32[320,128]{1,0:T(8,128)S(1)}, u32[]{:S(2)}, u32[]{:S(2)}) collective-permute-start(f32[320,128]{1,0:T(8,128)S(1)} %collective-permute-done.1.refs_2_), channel_id=1, source_target_pairs={{0,12},{4,0},{8,4},{12,8},{1,13},{5,1},{9,5},{13,9},{2,14},{6,2},{... | collective-permute-start | bytes 491528 | tf_op jit(solution)/shard_map/ppermute | solution.py:27
  15.5 9.1 %collective-permute-start.2 = (f32[160,128]{1,0:T(8,128)S(1)}, f32[160,128]{1,0:T(8,128)S(1)}, u32[]{:S(2)}, u32[]{:S(2)}) collective-permute-start(f32[160,128]{1,0:T(8,128)S(1)} %get-tuple-element.26), channel_id=1, source_target_pairs={{0,2},{1,3},{2,0},{3,1},{4,6},{5,7},{6,4},{7,5},{8,10},{9,11},{10,... | collective-permute-start | bytes 245768 | tf_op jit(solution)/shard_map/ppermute | solution.py:392
  16.6 8.8 %collective-permute-start.3 = (f32[160,128]{1,0:T(8,128)S(1)}, f32[160,128]{1,0:T(8,128)S(1)}, u32[]{:S(2)}, u32[]{:S(2)}) collective-permute-start(f32[160,128]{1,0:T(8,128)S(1)} %get-tuple-element.27), channel_id=1, source_target_pairs={{0,2},{1,3},{2,0},{3,1},{4,6},{5,7},{6,4},{7,5},{8,10},{9,11},{10,... | collective-permute-start | bytes 245768 | tf_op jit(solution)/shard_map/ppermute | solution.py:392
  24.5 8.3 %collective-permute-start.7 = (f32[160,128]{1,0:T(8,128)S(1)}, f32[160,128]{1,0:T(8,128)S(1)}, u32[]{:S(2)}, u32[]{:S(2)}) collective-permute-start(f32[160,128]{1,0:T(8,128)S(1)} %collective-permute-done.2.refs_3_), channel_id=1, source_target_pairs={{0,12},{4,0},{8,4},{12,8},{1,13},{5,1},{9,5},{13,9},{2,14},{6,2},{... | collective-permute-start | bytes 245768 | tf_op jit(solution)/shard_map/ppermute | solution.py:27
  25.4 7.5 %collective-permute-start.8 = (f32[160,128]{1,0:T(8,128)S(1)}, f32[160,128]{1,0:T(8,128)S(1)}, u32[]{:S(2)}, u32[]{:S(2)}) collective-permute-start(f32[160,128]{1,0:T(8,128)S(1)} %collective-permute-done.3.refs_4_), channel_id=1, source_target_pairs={{0,12},{4,0},{8,4},{12,8},{1,13},{5,1},{9,5},{13,9},{2,14},{6,2},{... | collective-permute-start | bytes 245768 | tf_op jit(solution)/shard_map/ppermute | solution.py:27
  26.0 0.7 %copy-start.4 = (s32[4]{0:T(128)S(1)}, s32[4]{0:T(128)}, u32[]{:S(2)}) copy-start(s32[4]{0:T(128)} %start_ref.1) | copy-start | bytes 52
  26.7 0.7 %copy-start.5 = (s32[4]{0:T(128)S(1)}, s32[4]{0:T(128)}, u32[]{:S(2)}) copy-start(s32[4]{0:T(128)} %stop_ref.1) | copy-start | bytes 52
  28.0 1.3 %copy-start.1 = (bf16[2,10,128,256]{3,2,1,0:T(8,128)(2,1)S(1)}, bf16[2,10,128,256]{3,2,1,0:T(8,128)(2,1)}, u32[]{:S(2)}) copy-start(bf16[2,10,128,256]{3,2,1,0:T(8,128)(2,1)} %constant.7.clone.refs_1_) | copy-start | bytes 3932164
  29.3 1.1 %copy-start.3 = (bf16[10,128,256]{2,1,0:T(8,128)(2,1)S(1)}, bf16[10,128,256]{2,1,0:T(8,128)(2,1)}, u32[]{:S(2)}) copy-start(bf16[10,128,256]{2,1,0:T(8,128)(2,1)} %constant.8.clone.refs_2_) | copy-start | bytes 1966084
  34.3 5.2 %collective-permute-start.9 = (f32[64,128]{1,0:T(8,128)S(1)}, f32[64,128]{1,0:T(8,128)S(1)}, u32[]{:S(2)}, u32[]{:S(2)}) collective-permute-start(f32[64,128]{1,0:T(8,128)S(1)} %get-tuple-element.32), channel_id=1, source_target_pairs={{0,2},{1,3},{2,0},{3,1},{4,6},{5,7},{6,4},{7,5},{8,10},{9,11},{10,... | collective-permute-start | bytes 98312 | tf_op jit(solution)/shard_map/ppermute | solution.py:392
  34.4 5.8 %collective-permute-start.10 = (f32[64,128]{1,0:T(8,128)S(1)}, f32[64,128]{1,0:T(8,128)S(1)}, u32[]{:S(2)}, u32[]{:S(2)}) collective-permute-start(f32[64,128]{1,0:T(8,128)S(1)} %get-tuple-element.33), channel_id=1, source_target_pairs={{0,3},{1,2},{2,1},{3,0},{4,7},{5,6},{6,5},{7,4},{8,11},{9,10},{10,... | collective-permute-start | bytes 98312 | tf_op jit(solution)/shard_map/ppermute | solution.py:392
  36.6 4.0 %collective-permute-start.11 = (f32[64,128]{1,0:T(8,128)S(1)}, f32[64,128]{1,0:T(8,128)S(1)}, u32[]{:S(2)}, u32[]{:S(2)}) collective-permute-start(f32[64,128]{1,0:T(8,128)S(1)} %get-tuple-element.34), channel_id=1, source_target_pairs={{0,1},{1,0},{2,3},{3,2},{4,5},{5,4},{6,7},{7,6},{8,9},{9,8},{10,11... | collective-permute-start | bytes 98312 | tf_op jit(solution)/shard_map/ppermute | solution.py:392

commit v2 on v1

--- a/solution.py
+++ b/solution.py
@@ -281,40 +281,53 @@
         weight_ref[m] = jnp.where(keep, 1.0 / (taps * inner), 0.0)
 
 
-def early_kernel(peers, ahead_ref, back_ref, weight_ref, *refs):
-    own_refs, sec_refs = refs[: peers + 1], refs[peers + 1 : 2 * peers]
-    mid_ref, same_ref, cross_ref = refs[2 * peers : 2 * peers + 3]
-    own_ref, own_turned_ref, sec_ref, sec_turned_ref = refs[2 * peers + 3 : -2]
-    own_mid_ref, own_back_ref = refs[-2:]
+def place(peers, chunk_refs, place_ref, turned_ref):
     me = lax.axis_index("line")
-    lines = own_ref.shape[0] // peers
-    inner = own_ref.shape[0] // TAPS
+    lines = place_ref.shape[0] // peers
     for q in range(peers):
         block = entry(senders(EXCHANGE[q - 1]), me) if q else me
         span = pl.ds(pl.multiple_of(block_of(me, block, peers) * lines, 8), lines)
-        own = own_refs[q][...] if q < peers - 1 else stacked(own_refs[q][...], own_refs[q + 1][...])
-        own_ref[span, :] = own
-        own_turned_ref[span, :] = turned(own)
-        if q == peers - 1:
-            sec_ref[span, :] = jnp.zeros((lines, LANES), jnp.float32)
-            sec_turned_ref[span, :] = jnp.zeros((lines, LANES), jnp.float32)
+        if q < len(chunk_refs):
+            values = chunk_refs[q][...]
+            place_ref[span, :], turned_ref[span, :] = values, turned(values)
         else:
-            sec = sec_refs[q][...]
-            sec_ref[span, :] = sec
-            sec_turned_ref[span, :] = turned(sec)
+            zeros = jnp.zeros((lines, LANES), jnp.float32)
+            place_ref[span, :], turned_ref[span, :] = zeros, zeros
+
+
+def bins_of(place_ref, turned_ref, ahead_ref, l):
+    span = pl.ds(l, place_ref.shape[0] // TAPS, stride=TAPS)
+    both = beside(*split_pair(stacked(place_ref[span, :], turned_ref[span, :])))
+    bins = product(ahead_ref[0, l], both) + product(ahead_ref[1, l], both)
+    return bins[:, :LANES] + bins[:, LANES:]
+
+
+def last_bins_of(first_ref, rest_ref, late_ref, l):
+    few = 2 * first_ref.shape[0] // TAPS
+    span = pl.ds(l, few // 2, stride=TAPS)
+    values = stacked(first_ref[span, :], rest_ref[span, :])
+    high, low = split_pair(stacked(values, turned(values)))
+    rest = jnp.zeros((late_ref.shape[2] - 6 * few, LANES), jnp.bfloat16)
+    return product(late_ref[l], stacked(high, low, high, rest))
+
+
+def first_kernel(peers, ahead_ref, *refs):
+    own_refs, (mid_ref, place_ref, turned_ref) = refs[: peers - 1], refs[peers - 1 :]
+    place(peers, own_refs, place_ref, turned_ref)
     for l in range(TAPS):
-        span = pl.ds(l, inner, stride=TAPS)
-        high, low = split_pair(
-            stacked(
-                beside(own_ref[span, :], sec_ref[span, :]),
-                beside(own_turned_ref[span, :], sec_turned_ref[span, :]),
-            )
-        )
-        table_high, table_low = ahead_ref[0, l], ahead_ref[1, l]
-        bins = product(table_high, high) + product(table_low, high) + product(table_high, low)
-        own_mid_ref[l] = bins[:, :LANES]
-        mid_ref[l] = bins[:, LANES:]
-
+        mid_ref[l] = bins_of(place_ref, turned_ref, ahead_ref, l)
+
+
+def early_kernel(
+    peers, ahead_ref, back_ref, late_ref, weight_ref, first_ref, last_ref, rest_ref, *refs
+):
+    sec_refs = refs[: peers - 1]
+    mid_ref, same_ref, cross_ref, place_ref, turned_ref, own_mid_ref, own_back_ref = refs[peers - 1 :]
+    for l in range(TAPS):
+        own_mid_ref[l] = first_ref[l] + last_bins_of(last_ref, rest_ref, late_ref, l)
+    place(peers, sec_refs, place_ref, turned_ref)
+    for l in range(TAPS):
+        mid_ref[l] = bins_of(place_ref, turned_ref, ahead_ref, l)
     spectral(own_mid_ref, weight_ref, own_back_ref)
     for l in range(TAPS):
         signal = signal_of(own_back_ref, back_ref, l) * (1.0 / LOOKS)
@@ -331,13 +344,8 @@
     total_ref, taps_ref, sum_ref = refs[peers:]
     me = lax.axis_index("line")
     inner = mid_ref.shape[1]
-    few = 2 * sec_ref.shape[0] // TAPS
-    rest = jnp.zeros((late_ref.shape[2] - 6 * few, LANES), jnp.bfloat16)
     for l in range(TAPS):
-        span = pl.ds(l, few // 2, stride=TAPS)
-        values = stacked(sec_ref[span, :], rest_ref[span, :])
-        high, low = split_pair(stacked(values, turned(values)))
-        total_ref[l] = mid_ref[l] + product(late_ref[l], stacked(high, low, high, rest))
+        total_ref[l] = mid_ref[l] + last_bins_of(sec_ref, rest_ref, late_ref, l)
     spectral(total_ref, weight_ref, taps_ref)
     for half in range(2):
         same, cross = None, None
@@ -418,15 +426,24 @@
         name="weights",
     )(band_start, band_stop)
     plane = pltpu.VMEM((peers * chunk_lines, LANES), f32)
+    first = pl.pallas_call(
+        functools.partial(first_kernel, peers),
+        out_shape=taps,
+        in_specs=[vmem] * peers,
+        out_specs=vmem,
+        scratch_shapes=[plane] * 2,
+        compiler_params=params,
+        name="first",
+    )(ahead_table, *own[:-2])
     middle, same, cross = pl.pallas_call(
         functools.partial(early_kernel, peers),
         out_shape=[taps] * 3,
-        in_specs=[vmem] * (2 * peers + 3),
+        in_specs=[vmem] * (peers + 6),
         out_specs=[vmem] * 3,
-        scratch_shapes=[plane] * 4 + [pltpu.VMEM(taps.shape, f32)] * 2,
+        scratch_shapes=[plane] * 2 + [pltpu.VMEM(taps.shape, f32)] * 2,
         compiler_params=params,
         name="early",
-    )(ahead_table, back_table, weight, *own, *sec[:-2])
+    )(ahead_table, back_table, late_table, weight, first, *own[-2:], *sec[:-2])
     looked = pl.pallas_call(
         functools.partial(late_kernel, peers),
         out_shape=[jax.ShapeDtypeStruct((out_lines, LANES), f32)] * peers,

time: 41.5 us -> 42.5 us (1.024)
  starting transfers between devices: 14 us -> 14.9 us
    ppermute x7, starting transfers between devices: 11.6 us -> 12.5 us  [exchange(): return lax.ppermute(values, 'line', list(enumerate(row)))]
    pallas_call x0 -> x1, Pallas kernels: none -> 0.74 us  [packed_step(): pl.pallas_call(functools.partial(first_kernel, peers), out_shape=taps, in...]
    pallas_call x1, Pallas kernels: 2.19 us -> 1.59 us  [packed_step(): pl.pallas_call(functools.partial(early_kernel, peers), out_shape=[taps] *...]
  transfers between devices with their start and end apart: 12 -> 12, of which waited for: 7 -> 7; matrix products, arithmetic and copies ran while one was open for 0% -> 0% of each run, Pallas kernels for 7% -> 8%
where the time goes in v2:
time: 42.5 us; the launch traced here: 42.2 us
  waiting for transfers between devices  16.7 us (39%)
  starting transfers between devices  14.9 us (35%)
  Pallas kernels  5.63 us (13%)
  local copies, waits for them, and re-layouts  4.9 us (12%)
    ppermute x7, waiting for transfers between devices, exchange(): return lax.ppermute(values, 'line', list(enumerate(row)))  16.7 us
    ppermute x7, starting transfers between devices, exchange(): return lax.ppermute(values, 'line', list(enumerate(row)))  12.5 us
    unnamed x12, local copies, waits for them, and re-layouts  4.9 us
    ppermute x5, starting transfers between devices, shifted(): lax.ppermute(shard, axis, [(i, (i + by) % size) for i in range(size)])  2.34 us
    pallas_call x1, Pallas kernels, packed_step(): pl.pallas_call(functools.partial(early_kernel, peers), out_shape=[taps] *...  1.59 us
    pallas_call x1, Pallas kernels, packed_step(): pl.pallas_call(functools.partial(late_kernel, peers), out_shape=[jax.Shap...  1.42 us
  transfers between devices with their start and end apart: 12, of which 7 were waited for; matrix products, arithmetic and copies ran while one was open for 0% of the time, Pallas kernels for 8%

profile of v2, /device:TPU:0, one launch (start us, length us, event | category | flops | bytes accessed | tf_op | source)
XLA Modules:
  0.0 42.2 jit_solution(7954558932482497024)
XLA Ops:
  0.0 0.0 copy-start
  0.0 0.0 copy-start.2
  0.0 1.2 %copy-done.2 = f32[1,2,256,320]{2,3,1,0:T(8,128)S(1)} copy-done((f32[1,2,256,320]{2,3,1,0:T(8,128)S(1)}, f32[1,2,256,320]{2,3,1,0:T(8,128)}, u32[]{:S(2)}) %copy-start.2) | copy-done | bytes 655384
  1.2 0.2 pack.1
  1.4 5.1 %collective-permute-start = (f32[320,128]{1,0:T(8,128)S(1)}, f32[320,128]{1,0:T(8,128)S(1)}, u32[]{:S(2)}, u32[]{:S(2)}) collective-permute-start(f32[320,128]{1,0:T(8,128)S(1)} %get-tuple-element.24), channel_id=1, source_target_pairs={{0,3},{1,2},{2,1},{3,0},{4,7},{5,6},{6,5},{7,4},{8,11},{9,10},{10,... | collective-permute-start | bytes 491528 | tf_op jit(solution)/shard_map/ppermute | solution.py:400
  6.6 0.0 collective-permute-start.1
  6.6 0.7 %collective-permute-start.4 = (f32[320,128]{1,0:T(8,128)S(1)}, f32[320,128]{1,0:T(8,128)S(1)}, u32[]{:S(2)}, u32[]{:S(2)}) collective-permute-start(f32[320,128]{1,0:T(8,128)S(1)} %get-tuple-element.23.refs_0_), channel_id=1, source_target_pairs={{0,12},{4,0},{8,4},{12,8},{1,13},{5,1},{9,5},{13,9},{2,14},{6,2},{... | collective-permute-start | bytes 491528 | tf_op jit(solution)/shard_map/ppermute | solution.py:27
  7.2 4.4 %collective-permute-done.refs_1_ = f32[320,128]{1,0:T(8,128)S(1)} collective-permute-done((f32[320,128]{1,0:T(8,128)S(1)}, f32[320,128]{1,0:T(8,128)S(1)}, u32[]{:S(2)}, u32[]{:S(2)}) %collective-permute-start) | collective-permute-done | bytes 163872 | tf_op jit(solution)/shard_map/ppermute | solution.py:400
  11.7 0.0 collective-permute-start.5
  11.7 2.7 %collective-permute-done.1.refs_2_ = f32[320,128]{1,0:T(8,128)S(1)} collective-permute-done((f32[320,128]{1,0:T(8,128)S(1)}, f32[320,128]{1,0:T(8,128)S(1)}, u32[]{:S(2)}, u32[]{:S(2)}) %collective-permute-start.1) | collective-permute-done | bytes 163872 | tf_op jit(solution)/shard_map/ppermute | solution.py:400
  14.4 1.1 %collective-permute-start.6 = (f32[320,128]{1,0:T(8,128)S(1)}, f32[320,128]{1,0:T(8,128)S(1)}, u32[]{:S(2)}, u32[]{:S(2)}) collective-permute-start(f32[320,128]{1,0:T(8,128)S(1)} %collective-permute-done.1.refs_2_), channel_id=1, source_target_pairs={{0,12},{4,0},{8,4},{12,8},{1,13},{5,1},{9,5},{13,9},{2,14},{6,2},{... | collective-permute-start | bytes 491528 | tf_op jit(solution)/shard_map/ppermute | solution.py:27
  15.5 1.1 %collective-permute-start.2 = (f32[160,128]{1,0:T(8,128)S(1)}, f32[160,128]{1,0:T(8,128)S(1)}, u32[]{:S(2)}, u32[]{:S(2)}) collective-permute-start(f32[160,128]{1,0:T(8,128)S(1)} %get-tuple-element.26), channel_id=1, source_target_pairs={{0,2},{1,3},{2,0},{3,1},{4,6},{5,7},{6,4},{7,5},{8,10},{9,11},{10,... | collective-permute-start | bytes 245768 | tf_op jit(solution)/shard_map/ppermute | solution.py:400
  16.6 1.8 %collective-permute-start.3 = (f32[160,128]{1,0:T(8,128)S(1)}, f32[160,128]{1,0:T(8,128)S(1)}, u32[]{:S(2)}, u32[]{:S(2)}) collective-permute-start(f32[160,128]{1,0:T(8,128)S(1)} %get-tuple-element.27), channel_id=1, source_target_pairs={{0,2},{1,3},{2,0},{3,1},{4,6},{5,7},{6,4},{7,5},{8,10},{9,11},{10,... | collective-permute-start | bytes 245768 | tf_op jit(solution)/shard_map/ppermute | solution.py:400
  18.4 6.1 %collective-permute-done.2.last_ref = f32[160,128]{1,0:T(8,128)S(1)} collective-permute-done((f32[160,128]{1,0:T(8,128)S(1)}, f32[160,128]{1,0:T(8,128)S(1)}, u32[]{:S(2)}, u32[]{:S(2)}) %collective-permute-start.2) | collective-permute-done | bytes 81952 | tf_op jit(solution)/shard_map/ppermute | solution.py:400
  24.5 0.0 collective-permute-start.7
  24.5 0.9 %collective-permute-done.3.rest_ref = f32[160,128]{1,0:T(8,128)S(1)} collective-permute-done((f32[160,128]{1,0:T(8,128)S(1)}, f32[160,128]{1,0:T(8,128)S(1)}, u32[]{:S(2)}, u32[]{:S(2)}) %collective-permute-start.3) | collective-permute-done | bytes 81952 | tf_op jit(solution)/shard_map/ppermute | solution.py:400
  25.4 0.6 %collective-permute-start.8 = (f32[160,128]{1,0:T(8,128)S(1)}, f32[160,128]{1,0:T(8,128)S(1)}, u32[]{:S(2)}, u32[]{:S(2)}) collective-permute-start(f32[160,128]{1,0:T(8,128)S(1)} %collective-permute-done.3.rest_ref), channel_id=1, source_target_pairs={{0,12},{4,0},{8,4},{12,8},{1,13},{5,1},{9,5},{13,9},{2,14},{6,2},{... | collective-permute-start | bytes 245768 | tf_op jit(solution)/shard_map/ppermute | solution.py:27
  26.0 0.0 copy-start.4
  26.0 0.7 %copy-done.4 = s32[4]{0:T(128)S(1)} copy-done((s32[4]{0:T(128)S(1)}, s32[4]{0:T(128)}, u32[]{:S(2)}) %copy-start.4) | copy-done | bytes 40
  26.7 0.0 copy-start.5
  26.7 0.7 %copy-done.5 = s32[4]{0:T(128)S(1)} copy-done((s32[4]{0:T(128)S(1)}, s32[4]{0:T(128)}, u32[]{:S(2)}) %copy-start.5) | copy-done | bytes 40
  27.3 0.7 %weights.1.weight_ref = f32[10,128,128]{2,1,0:T(8,128)S(1)} custom-call(s32[4]{0:T(128)S(1)} %copy-done.4, s32[4]{0:T(128)S(1)} %copy-done.5), custom_call_target="tpu_custom_call" | custom-call | tf_op jit(solution)/shard_map/weights/pallas_call | solution.py:420
  28.0 0.0 copy-done
  28.0 0.0 copy-start.1
  28.0 1.3 %copy-done.1 = bf16[2,10,128,256]{3,2,1,0:T(8,128)(2,1)S(1)} copy-done((bf16[2,10,128,256]{3,2,1,0:T(8,128)(2,1)S(1)}, bf16[2,10,128,256]{3,2,1,0:T(8,128)(2,1)}, u32[]{:S(2)}) %copy-start.1) | copy-done | bytes 1310744
  29.3 0.0 copy-start.3
  29.3 1.1 %copy-done.3 = bf16[10,128,256]{2,1,0:T(8,128)(2,1)S(1)} copy-done((bf16[10,128,256]{2,1,0:T(8,128)(2,1)S(1)}, bf16[10,128,256]{2,1,0:T(8,128)(2,1)}, u32[]{:S(2)}) %copy-start.3) | copy-done | bytes 655384
  30.4 0.2 tables.1
  30.6 0.7 %first.1.first_ref = f32[10,128,128]{2,1,0:T(8,128)S(1)} custom-call(bf16[2,10,128,256]{3,2,1,0:T(8,128)(2,1)S(1)} %get-tuple-element.22.ahead_ref, f32[320,128]{1,0:T(8,128)S(1)} %get-tuple-element.23.refs_0_, f32[320,128]{1,0:T(8,128)S(1)} %collective-permute-done.refs_1_, f32[320,128]{1,0:T(8,128)S(1)} %collective-permute-done.1.refs_2_), custom_call_target="tpu_custom_call" | custom-call | tf_op jit(solution)/shard_map/first/pallas_call | solution.py:429
  31.4 0.0 collective-permute-done.4.refs_0_
  31.4 0.0 collective-permute-done.5.refs_1_
  31.4 0.0 collective-permute-done.6.refs_2_
  31.4 1.6 %early.1 = (f32[10,128,128]{2,1,0:T(8,128)S(1)}, f32[10,128,128]{2,1,0:T(8,128)S(1)}, f32[10,128,128]{2,1,0:T(8,128)S(1)}) custom-call(bf16[2,10,128,256]{3,2,1,0:T(8,128)(2,1)S(1)} %get-tuple-element.22.ahead_ref, bf16[2,10,128,256]{3,2,1,0:T(8,128)(2,1)S(1)} %get-tuple-element.21.back_ref, bf16[10,128,256]{2,1,0:T(8,128)(2,1)S(1)} %get-tuple-element.20.late_ref, ...), custom_call_target="tpu_custom_call" | custom-call | tf_op jit(solution)/shard_map/early/pallas_call | solution.py:438
  33.0 0.0 collective-permute-done.7.sec_ref
  33.0 0.0 collective-permute-done.8.rest_ref
  33.0 1.4 %late.1 = (f32[64,128]{1,0:T(8,128)S(1)}, f32[64,128]{1,0:T(8,128)S(1)}, f32[64,128]{1,0:T(8,128)S(1)}, f32[64,128]{1,0:T(8,128)S(1)}) custom-call(bf16[10,128,256]{2,1,0:T(8,128)(2,1)S(1)} %get-tuple-element.20.late_ref, bf16[2,10,128,256]{3,2,1,0:T(8,128)(2,1)S(1)} %get-tuple-element.21.back_ref, f32[10,128,128]{2,1,0:T(8,128)S(1)} %get-tuple-element.28.mid_ref, ...), custom_call_target="tpu_custom_call" | custom-call | tf_op jit(solution)/shard_map/late/pallas_call | solution.py:447
  34.4 2.2 %collective-permute-start.10 = (f32[64,128]{1,0:T(8,128)S(1)}, f32[64,128]{1,0:T(8,128)S(1)}, u32[]{:S(2)}, u32[]{:S(2)}) collective-permute-start(f32[64,128]{1,0:T(8,128)S(1)} %get-tuple-element.33), channel_id=1, source_target_pairs={{0,3},{1,2},{2,1},{3,0},{4,7},{5,6},{6,5},{7,4},{8,11},{9,10},{10,... | collective-permute-start | bytes 98312 | tf_op jit(solution)/shard_map/ppermute | solution.py:400
  36.6 0.0 collective-permute-start.11
  36.6 2.3 %collective-permute-start.9 = (f32[64,128]{1,0:T(8,128)S(1)}, f32[64,128]{1,0:T(8,128)S(1)}, u32[]{:S(2)}, u32[]{:S(2)}) collective-permute-start(f32[64,128]{1,0:T(8,128)S(1)} %get-tuple-element.32), channel_id=1, source_target_pairs={{0,2},{1,3},{2,0},{3,1},{4,6},{5,7},{6,4},{7,5},{8,10},{9,11},{10,... | collective-permute-start | bytes 98312 | tf_op jit(solution)/shard_map/ppermute | solution.py:400
  38.9 1.3 %collective-permute-done.10.refs_2_ = f32[64,128]{1,0:T(8,128)S(1)} collective-permute-done((f32[64,128]{1,0:T(8,128)S(1)}, f32[64,128]{1,0:T(8,128)S(1)}, u32[]{:S(2)}, u32[]{:S(2)}) %collective-permute-start.10) | collective-permute-done | bytes 32800 | tf_op jit(solution)/shard_map/ppermute | solution.py:400
  40.2 0.4 collective-permute-done.11.refs_3_
  40.6 0.9 %collective-permute-done.9.refs_1_ = f32[64,128]{1,0:T(8,128)S(1)} collective-permute-done((f32[64,128]{1,0:T(8,128)S(1)}, f32[64,128]{1,0:T(8,128)S(1)}, u32[]{:S(2)}, u32[]{:S(2)}) %collective-permute-start.9) | collective-permute-done | bytes 32800 | tf_op jit(solution)/shard_map/ppermute | solution.py:400
  41.5 0.8 %unpack.1 = f32[2,64,256]{2,1,0:T(8,128)} custom-call(f32[64,128]{1,0:T(8,128)S(1)} %get-tuple-element.31.refs_0_, f32[64,128]{1,0:T(8,128)S(1)} %collective-permute-done.9.refs_1_, f32[64,128]{1,0:T(8,128)S(1)} %collective-permute-done.10.refs_2_, f32[64,128]{1,0:T(8,128)S(1)} %collective-permute-done.11.refs_3_), custom_call_target="tpu_custom_call" | custom-call | tf_op jit(solution)/shard_map/unpack/pallas_call | solution.py:461
Async XLA Ops:
  0.0 28.0 %copy-start = (bf16[2,10,128,256]{3,2,1,0:T(8,128)(2,1)S(1)}, bf16[2,10,128,256]{3,2,1,0:T(8,128)(2,1)}, u32[]{:S(2)}) copy-start(bf16[2,10,128,256]{3,2,1,0:T(8,128)(2,1)} %constant.6.clone.refs_0_) | copy-start | bytes 3932164
  0.0 1.2 %copy-start.2 = (f32[1,2,256,320]{2,3,1,0:T(8,128)S(1)}, f32[1,2,256,320]{2,3,1,0:T(8,128)}, u32[]{:S(2)}) copy-start(f32[1,2,256,320]{2,3,1,0:T(8,128)} %param.6) | copy-start | bytes 1966084
  1.4 10.2 %collective-permute-start = (f32[320,128]{1,0:T(8,128)S(1)}, f32[320,128]{1,0:T(8,128)S(1)}, u32[]{:S(2)}, u32[]{:S(2)}) collective-permute-start(f32[320,128]{1,0:T(8,128)S(1)} %get-tuple-element.24), channel_id=1, source_target_pairs={{0,3},{1,2},{2,1},{3,0},{4,7},{5,6},{6,5},{7,4},{8,11},{9,10},{10,... | collective-permute-start | bytes 491528 | tf_op jit(solution)/shard_map/ppermute | solution.py:400
  6.6 7.8 %collective-permute-start.1 = (f32[320,128]{1,0:T(8,128)S(1)}, f32[320,128]{1,0:T(8,128)S(1)}, u32[]{:S(2)}, u32[]{:S(2)}) collective-permute-start(f32[320,128]{1,0:T(8,128)S(1)} %get-tuple-element.25), channel_id=1, source_target_pairs={{0,1},{1,0},{2,3},{3,2},{4,5},{5,4},{6,7},{7,6},{8,9},{9,8},{10,11... | collective-permute-start | bytes 491528 | tf_op jit(solution)/shard_map/ppermute | solution.py:400
  6.6 24.8 %collective-permute-start.4 = (f32[320,128]{1,0:T(8,128)S(1)}, f32[320,128]{1,0:T(8,128)S(1)}, u32[]{:S(2)}, u32[]{:S(2)}) collective-permute-start(f32[320,128]{1,0:T(8,128)S(1)} %get-tuple-element.23.refs_0_), channel_id=1, source_target_pairs={{0,12},{4,0},{8,4},{12,8},{1,13},{5,1},{9,5},{13,9},{2,14},{6,2},{... | collective-permute-start | bytes 491528 | tf_op jit(solution)/shard_map/ppermute | solution.py:27
  11.7 19.7 %collective-permute-start.5 = (f32[320,128]{1,0:T(8,128)S(1)}, f32[320,128]{1,0:T(8,128)S(1)}, u32[]{:S(2)}, u32[]{:S(2)}) collective-permute-start(f32[320,128]{1,0:T(8,128)S(1)} %collective-permute-done.refs_1_), channel_id=1, source_target_pairs={{0,12},{4,0},{8,4},{12,8},{1,13},{5,1},{9,5},{13,9},{2,14},{6,2},{... | collective-permute-start | bytes 491528 | tf_op jit(solution)/shard_map/ppermute | solution.py:27
  14.4 17.0 %collective-permute-start.6 = (f32[320,128]{1,0:T(8,128)S(1)}, f32[320,128]{1,0:T(8,128)S(1)}, u32[]{:S(2)}, u32[]{:S(2)}) collective-permute-start(f32[320,128]{1,0:T(8,128)S(1)} %collective-permute-done.1.refs_2_), channel_id=1, source_target_pairs={{0,12},{4,0},{8,4},{12,8},{1,13},{5,1},{9,5},{13,9},{2,14},{6,2},{... | collective-permute-start | bytes 491528 | tf_op jit(solution)/shard_map/ppermute | solution.py:27
  15.5 9.1 %collective-permute-start.2 = (f32[160,128]{1,0:T(8,128)S(1)}, f32[160,128]{1,0:T(8,128)S(1)}, u32[]{:S(2)}, u32[]{:S(2)}) collective-permute-start(f32[160,128]{1,0:T(8,128)S(1)} %get-tuple-element.26), channel_id=1, source_target_pairs={{0,2},{1,3},{2,0},{3,1},{4,6},{5,7},{6,4},{7,5},{8,10},{9,11},{10,... | collective-permute-start | bytes 245768 | tf_op jit(solution)/shard_map/ppermute | solution.py:400
  16.6 8.8 %collective-permute-start.3 = (f32[160,128]{1,0:T(8,128)S(1)}, f32[160,128]{1,0:T(8,128)S(1)}, u32[]{:S(2)}, u32[]{:S(2)}) collective-permute-start(f32[160,128]{1,0:T(8,128)S(1)} %get-tuple-element.27), channel_id=1, source_target_pairs={{0,2},{1,3},{2,0},{3,1},{4,6},{5,7},{6,4},{7,5},{8,10},{9,11},{10,... | collective-permute-start | bytes 245768 | tf_op jit(solution)/shard_map/ppermute | solution.py:400
  24.5 8.5 %collective-permute-start.7 = (f32[160,128]{1,0:T(8,128)S(1)}, f32[160,128]{1,0:T(8,128)S(1)}, u32[]{:S(2)}, u32[]{:S(2)}) collective-permute-start(f32[160,128]{1,0:T(8,128)S(1)} %collective-permute-done.2.last_ref), channel_id=1, source_target_pairs={{0,12},{4,0},{8,4},{12,8},{1,13},{5,1},{9,5},{13,9},{2,14},{6,2},{... | collective-permute-start | bytes 245768 | tf_op jit(solution)/shard_map/ppermute | solution.py:27
  25.4 7.6 %collective-permute-start.8 = (f32[160,128]{1,0:T(8,128)S(1)}, f32[160,128]{1,0:T(8,128)S(1)}, u32[]{:S(2)}, u32[]{:S(2)}) collective-permute-start(f32[160,128]{1,0:T(8,128)S(1)} %collective-permute-done.3.rest_ref), channel_id=1, source_target_pairs={{0,12},{4,0},{8,4},{12,8},{1,13},{5,1},{9,5},{13,9},{2,14},{6,2},{... | collective-permute-start | bytes 245768 | tf_op jit(solution)/shard_map/ppermute | solution.py:27
  26.0 0.7 %copy-start.4 = (s32[4]{0:T(128)S(1)}, s32[4]{0:T(128)}, u32[]{:S(2)}) copy-start(s32[4]{0:T(128)} %start_ref.1) | copy-start | bytes 52
  26.7 0.7 %copy-start.5 = (s32[4]{0:T(128)S(1)}, s32[4]{0:T(128)}, u32[]{:S(2)}) copy-start(s32[4]{0:T(128)} %stop_ref.1) | copy-start | bytes 52
  28.0 1.3 %copy-start.1 = (bf16[2,10,128,256]{3,2,1,0:T(8,128)(2,1)S(1)}, bf16[2,10,128,256]{3,2,1,0:T(8,128)(2,1)}, u32[]{:S(2)}) copy-start(bf16[2,10,128,256]{3,2,1,0:T(8,128)(2,1)} %constant.7.clone.refs_1_) | copy-start | bytes 3932164
  29.3 1.1 %copy-start.3 = (bf16[10,128,256]{2,1,0:T(8,128)(2,1)S(1)}, bf16[10,128,256]{2,1,0:T(8,128)(2,1)}, u32[]{:S(2)}) copy-start(bf16[10,128,256]{2,1,0:T(8,128)(2,1)} %constant.8.clone.refs_2_) | copy-start | bytes 1966084
  34.4 5.8 %collective-permute-start.10 = (f32[64,128]{1,0:T(8,128)S(1)}, f32[64,128]{1,0:T(8,128)S(1)}, u32[]{:S(2)}, u32[]{:S(2)}) collective-permute-start(f32[64,128]{1,0:T(8,128)S(1)} %get-tuple-element.33), channel_id=1, source_target_pairs={{0,3},{1,2},{2,1},{3,0},{4,7},{5,6},{6,5},{7,4},{8,11},{9,10},{10,... | collective-permute-start | bytes 98312 | tf_op jit(solution)/shard_map/ppermute | solution.py:400
  36.6 3.9 %collective-permute-start.11 = (f32[64,128]{1,0:T(8,128)S(1)}, f32[64,128]{1,0:T(8,128)S(1)}, u32[]{:S(2)}, u32[]{:S(2)}) collective-permute-start(f32[64,128]{1,0:T(8,128)S(1)} %get-tuple-element.34), channel_id=1, source_target_pairs={{0,1},{1,0},{2,3},{3,2},{4,5},{5,4},{6,7},{7,6},{8,9},{9,8},{10,11... | collective-permute-start | bytes 98312 | tf_op jit(solution)/shard_map/ppermute | solution.py:400
  36.6 4.8 %collective-permute-start.9 = (f32[64,128]{1,0:T(8,128)S(1)}, f32[64,128]{1,0:T(8,128)S(1)}, u32[]{:S(2)}, u32[]{:S(2)}) collective-permute-start(f32[64,128]{1,0:T(8,128)S(1)} %get-tuple-element.32), channel_id=1, source_target_pairs={{0,2},{1,3},{2,0},{3,1},{4,6},{5,7},{6,4},{7,5},{8,10},{9,11},{10,... | collective-permute-start | bytes 98312 | tf_op jit(solution)/shard_map/ppermute | solution.py:400
